TPU v7x, 128 devices: a whole 4x4x4 slice. The times are simulated.
128 devices in a mesh: rows: 16 (over y_hi, z, core), tiles: 8 (over y_lo, x).
Axes of the slice: x: 4, y: 4 (y_hi: 2, y_lo: 2; y = y_hi * 2 + y_lo), z: 4, core: 2. Of those that a mesh axis runs over, the one named last changes fastest.
Arguments:
- features: bfloat16 [16384, 16384], P(('rows', 'tiles')), as said below
- row_salt: int32 [16384], P(('rows', 'tiles')), may hold values from 0 to 32767
- column_multiplier: int32 [16384], replicated, may hold values from 1 to 32767
- column_offset: int32 [16384], replicated, may hold values from 0 to 65520
- thresholds: int32 [16384], replicated, may hold values from 16000 to 65520
Outputs:
- similarity: float32 [256, 16384], P('rows', 'tiles')
Inputs may be any that keep to these rules, and one draw needn't show every extreme that they name: `features`: Real-valued entries of order one.
All inputs are finite; a program needn't handle non-finite values.
Results may differ from a plain program's by a relative error of at most 0.0028.
Values sent between devices are 32-bit elements; how exact they have to be, the bound alone decides.
No kernel may reach another device: no remote copies, remote signals or barrier semaphores. Data moves between devices by JAX's collectives and lax.ppermute only.
A program may use at most 64 MiB of HBM per device.

v0:
```python
import jax
import jax.numpy as jnp
from jax import lax
from jax.sharding import PartitionSpec as P

N = 16384
WIN = 256


def sample_block(block, salts, column_multiplier, column_offset, thresholds):
    hashed = (salts[:, None] * column_multiplier[None, :] + column_offset[None, :]) % 65521
    weight = lax.rsqrt(thresholds.astype(jnp.float32) / 65521.0)
    values = block.astype(jnp.float32) * weight[None, :]
    return jnp.where(hashed < thresholds[None, :], values, jnp.zeros_like(values)).astype(
        jnp.bfloat16
    )


def inner_product(left, right):
    return lax.dot_general(
        left, right, (((0,), (0,)), ((), ())), preferred_element_type=jnp.float32
    )


def shards(features, row_salt, column_multiplier, column_offset, thresholds):
    wide = features.astype(jnp.float32)
    squares = lax.psum(jnp.sum(wide * wide, axis=0), ("rows", "tiles"))
    norms = jnp.sqrt(squares + 1e-06)
    sampled = sample_block(features, row_salt, column_multiplier, column_offset, thresholds)
    queries = sampled[:, :WIN]
    count_rows = lax.axis_size("rows")
    count_tiles = lax.axis_size("tiles")
    block_rows = WIN // count_rows
    block_cols = N // count_tiles
    partial_value = inner_product(queries, sampled)
    halfway = lax.psum_scatter(partial_value, "tiles", scatter_dimension=1, tiled=True)
    tile = lax.psum_scatter(halfway, "rows", scatter_dimension=0, tiled=True)
    query_norms = lax.dynamic_slice_in_dim(
        norms, lax.axis_index("rows") * block_rows, block_rows, 0
    )
    column_norms = lax.dynamic_slice_in_dim(
        norms, lax.axis_index("tiles") * block_cols, block_cols, 0
    )
    return tile / (query_norms[:, None] * column_norms[None, :])


def solution(mesh):
    placed = (P(("rows", "tiles"), None), P(("rows", "tiles")), P(), P(), P())
    return jax.shard_map(
        shards, mesh=mesh, in_specs=placed, out_specs=P("rows", "tiles"), check_vma=False
    )
```

profile of v0, /device:TPU:1, one launch (start us, length us, event | category | flops | bytes accessed | tf_op | source)
XLA Modules:
  0.0 318.3 jit_solution(5690170771330322499)
XLA Ops:
  7.4 0.0 reduce-scatter.3.cloned.1.call-start
  7.4 0.9 multiply_rsqrt_fusion
  8.2 9.9 %fusion.2 = (f32[16384]{0:T(1024)}, bf16[128,16384]{1,0:T(8,128)(2,1)S(1)}) fusion(bf16[128,16384]{1,0:T(8,128)(2,1)} %param.5, f32[16384]{0:T(1024)S(1)} %multiply_rsqrt_fusion, s32[16384]{0:T(1024)} %param.9, s32[16384]{0:T(1024)} %param.8, s32[16384]{0:T(1024)} %param.7, s32[128]{0:T(128)} %param.6), kind=kLoop, calls=%fused_computation.5 | loop fusion | flops 31440896 | bytes 8716800 | tf_op jit(solution)/shard_map/reduce_sum | solution.py:27
  18.1 8.1 %fusion.7 = f32[256,16384]{1,0:T(8,128)} fusion(bf16[128,16384]{1,0:T(8,128)(2,1)S(1)} %get-tuple-element.6), kind=kOutput, calls=%fused_computation.12 | convolution fusion | flops 1073741824 | bytes 21037056 | tf_op jit(solution)/shard_map/dot_general | solution.py:20
  26.2 0.0 reduce-scatter.3.cloned.1.call-update
  26.2 0.0 all-reduce.2.cloned.1.call-start
  26.2 0.5 all-reduce.2.cloned.1.call-update
  26.8 0.0 reduce-scatter.5.cloned.1.call-start
  26.8 174.5 %reduce-scatter.3.cloned.1.call-done = f32[256,2048]{1,0:T(8,128)} async-done(((f32[256,16384]{1,0:T(8,128)}), f32[256,2048]{1,0:T(8,128)}) %reduce-scatter.3.cloned.1.call-update) | async-done | bytes 2097168 | tf_op jit(solution)/shard_map/reduce_scatter | solution.py:36
  201.3 0.0 reduce-scatter.5.cloned.1.call-update
  201.3 106.9 %all-reduce.2.cloned.1.call-done = f32[16384]{0:T(1024)} async-done(((f32[16384]{0:T(1024)}), f32[16384]{0:T(1024)}) %all-reduce.2.cloned.1.call-update) | async-done | bytes 65552 | tf_op jit(solution)/shard_map/psum | solution.py:27
  308.3 0.9 add_sqrt_fusion
  309.1 0.1 dynamic_slice.6
  309.2 0.0 reduce-scatter.5.cloned.1.call-done
  309.2 1.7 multiply_divide_fusion
  (1 shorter events, 0.0 us)
Async XLA Ops:
  7.4 193.9 %reduce-scatter.3.cloned.1.call-start = ((), (), s32[]{:S(2)}) async-start(), calls=%async_computation.2 | async-start | bytes 18874368 | tf_op jit(solution)/shard_map/reduce_scatter | solution.py:36
  26.2 282.1 %all-reduce.2.cloned.1.call-start = ((), (), s32[]{:S(2)}) async-start(), calls=%async_computation.4 | async-start | bytes 131072 | tf_op jit(solution)/shard_map/psum | solution.py:27
  26.8 282.5 %reduce-scatter.5.cloned.1.call-start = ((), (), s32[]{:S(2)}) async-start(), calls=%async_computation.3 | async-start | bytes 2228224 | tf_op jit(solution)/shard_map/reduce_scatter | solution.py:37
Sparse Core Ops, SparseCore 0:
  26.3 174.9 reduce-scatter.2
  205.2 67.8 reduce-scatter.4
Sparse Core Ops, SparseCore 1:
  31.4 276.8 all-reduce.1
where the time goes:
time: 319 us; the launch traced here: 318 us
  waiting for transfers between devices  282 us (88%)
  between operations  14.9 us (5%)
  other arithmetic  13.2 us (4%)
  matrix products  8.08 us (3%)
    reduce_scatter x1, waiting for transfers between devices, shards(): lax.psum_scatter(partial_value, 'tiles', scatter_dimension=1, tiled=True)  174 us
    psum x1, waiting for transfers between devices, shards(): squares = lax.psum(jnp.sum(wide * wide, axis=0), ('rows', 'tiles'))  107 us
    reduce_sum x1, other arithmetic, shards(): squares = lax.psum(jnp.sum(wide * wide, axis=0), ('rows', 'tiles'))  9.86 us
    dot_general x1, matrix products, inner_product(): lax.dot_general(left, right, (((0,), (0,)), ((), ())), preferred_element_...  8.08 us
  transfers between devices with their start and end apart: 3, of which 2 were waited for; matrix products, arithmetic and copies ran while one was open for 0% of the time, Pallas kernels for 0%

commit v1 on v0

v1 whole, which is shorter than its diff:
```python
import functools

import jax
import jax.numpy as jnp
from jax import lax
from jax.experimental import pallas as pl
from jax.experimental.pallas import tpu as pltpu
from jax.sharding import PartitionSpec as P

AXES = ("rows", "tiles")
LANES = 128
PRIME = 65521
SLOT_TILES = ((0, 1, 2), (3, 4, 5), (6, 7))
SLOT_ROWS = (96, 96, 80)
ALL_ROWS = sum(SLOT_ROWS)


def place(index):
    rows, tiles = divmod(index, 8)
    return [tiles & 3, (rows >> 3) * 2 + (tiles >> 2), (rows >> 1) & 3], rows & 1


def index_of(chip, core):
    x, y, z = chip
    return (((y >> 1) << 3) | (z << 1) | core) * 8 + ((y & 1) << 2 | x)


def gray(v):
    return v ^ (v >> 1)


def flip(index, first, last):
    chip, core = place(index)
    for axis in range(3):
        mask = first[axis] << core | last[axis] << (1 - core)
        chip[axis] = gray(gray(chip[axis]) ^ mask)
    return index_of(chip, core)


def moves(first, last):
    return [(i, flip(i, first, last)) for i in range(128)]


def axis_bits(axis):
    return [int(a == axis % 3) for a in range(3)]


def my_place():
    rows = lax.axis_index("rows")
    tile = lax.axis_index("tiles")
    return rows & 1, rows >> 1, tile


def tile_at(core, tile, c, xa, xb):
    high = jnp.where(core == 0, xb, xa)
    return tile ^ (c * 4 + high * 2 + (xa ^ xb))


def weight_of(threshold):
    return lax.rsqrt(threshold.astype(jnp.float32) / 65521.0)


def fold(v):
    return v - (v >> 16) * PRIME


def sample(values, salt, multiplier, offset, threshold, weight):
    residue = fold(fold(salt * multiplier + offset))
    keep = (residue < threshold) | (residue >= PRIME)
    return jnp.where(keep, values * weight, 0.0).astype(jnp.bfloat16)


def call(kernel, out_shape, in_spaces, scratch=(), limit=16, flops=1_000_000, nbytes=1 << 20):
    spaces = {"v": pltpu.VMEM, "h": pltpu.HBM}
    return pl.pallas_call(
        kernel,
        out_shape=[jax.ShapeDtypeStruct(s, d) for s, d in out_shape],
        in_specs=[pl.BlockSpec(memory_space=spaces[s]) for s in in_spaces],
        out_specs=[pl.BlockSpec(memory_space=pltpu.VMEM)] * len(out_shape),
        scratch_shapes=list(scratch),
        compiler_params=pltpu.CompilerParams(vmem_limit_bytes=limit << 20),
        cost_estimate=pl.CostEstimate(flops=flops, bytes_accessed=nbytes, transcendentals=0),
    )


ORDER = [(xa, c, xb) for xa in (1, 0) for c in (0, 1) for xb in (0, 1)]


def cast_kernel(feat, salt, outq, out0s, out1, out2, out0k, block, queries, salts, sems):
    core, _, tile = my_place()
    copies = [
        pltpu.make_async_copy(feat.at[:, 0:256], queries, sems.at[8]),
        pltpu.make_async_copy(salt, salts, sems.at[9]),
    ]
    for i, (xa, c, xb) in enumerate(ORDER):
        start = pl.multiple_of(tile_at(1 - core, tile, c, xa, xb) * 2048 + (1 - core) * 1024, 1024)
        copies.append(
            pltpu.make_async_copy(feat.at[:, pl.ds(start, 1024)], block.at[i], sems.at[i])
        )
    for copy in copies:
        copy.start()
    copies[0].wait()
    copies[1].wait()
    outq[0:128, :] = queries[...].astype(jnp.float32)
    row = jnp.broadcast_to(salts[...].astype(jnp.float32), (8, LANES))
    outq[128:136, 0:128] = row
    outq[128:136, 128:256] = row
    for i in range(8):
        copies[2 + i].wait()
        out0 = out0s if i < 4 else out0k
        out0[i % 4] = block[i, :, 0:384].astype(jnp.float32)
        out1[i] = block[i, :, 384:768].astype(jnp.float32)
        out2[i] = block[i, :, 768:1024].astype(jnp.float32)


def cast_call(features, salt):
    f32 = jnp.float32
    return call(
        cast_kernel,
        [
            ((136, 256), f32),
            ((4, 128, 384), f32),
            ((8, 128, 384), f32),
            ((8, 128, 256), f32),
            ((4, 128, 384), f32),
        ],
        "hh",
        scratch=[
            pltpu.VMEM((8, 128, 1024), jnp.bfloat16),
            pltpu.VMEM((128, 256), jnp.bfloat16),
            pltpu.VMEM((1, 128), jnp.int32),
            pltpu.SemaphoreType.DMA((10,)),
        ],
        nbytes=6 << 20,
    )(features, salt)


def column_of(row):
    return jnp.transpose(jnp.broadcast_to(row, (128, 128)))


def block_row(base, l):
    return pl.ds(base + l, 1)


def own_kernel(feat, salt, mult, offs, thr, cols, squares, block, sems):
    core, _, tile = my_place()
    salts = column_of(salt[...])
    copies, tiles = [], []
    for i, (xa, c, xb) in enumerate(ORDER):
        at = tile_at(core, tile, c, xa, xb)
        tiles.append(at)
        start = pl.multiple_of(at * 2048 + core * 1024, 1024)
        copies.append(
            pltpu.make_async_copy(feat.at[:, pl.ds(start, 1024)], block.at[i], sems.at[i])
        )
        copies[i].start()
    for i in range(8):
        copies[i].wait()
        base = tiles[i] * 16 + core * 8
        for l in range(8):
            m, o, t = (ref[block_row(base, l), :] for ref in (mult, offs, thr))
            lanes = slice(l * 128, (l + 1) * 128)
            x = block[i, :, lanes].astype(jnp.float32)
            squares[i, l : l + 1, :] = jnp.sum(x * x, axis=0, keepdims=True)
            cols[i, :, lanes] = sample(x, salts, m, o, t, weight_of(t))


def own_call(features, salt, mult, offs, thr):
    return call(
        own_kernel,
        [((8, 128, 1024), jnp.bfloat16), ((8, 8, 128), jnp.float32)],
        "hvvvv",
        scratch=[
            pltpu.VMEM((8, 128, 1024), jnp.bfloat16),
            pltpu.SemaphoreType.DMA((8,)),
        ],
        flops=20_000_000,
        nbytes=4 << 20,
    )(features, salt, mult, offs, thr)


def query_kernel(feat, other, salt, mult, offs, thr, q_out, salt_out, sq_out, q_all, queries, sem):
    core, pair, _ = my_place()
    copy = pltpu.make_async_copy(feat.at[:, 0:256], queries, sem)
    copy.start()
    salts = (column_of(salt[...]), column_of(other[128:129, 0:128].astype(jnp.int32)))
    salt_out[...] = salts[1]
    sq_out[...] = jnp.zeros_like(sq_out)
    copy.wait()
    for l in range(2):
        lanes = slice(l * 128, (l + 1) * 128)
        m, o, t = (ref[l : l + 1, :] for ref in (mult, offs, thr))
        w = weight_of(t)
        total = None
        for u in range(2):
            source = queries if u == 0 else other
            x = source[0:128, lanes].astype(jnp.float32)
            part = jnp.sum(x * x, axis=0, keepdims=True)
            total = part if total is None else total + part
            value = sample(x, salts[u], m, o, t, w).astype(jnp.float32)
            q_all[lanes, u * 128 : (u + 1) * 128] = jnp.transpose(value).astype(jnp.bfloat16)
        sq_out[l : l + 1, :] = total
    for c in range(2):
        for group in range(8):
            ya, za, zb = group >> 2, group >> 1 & 1, group & 1
            z_high = jnp.where(core == 0, zb, za)
            y_high = jnp.where(core == 0, c ^ ya, ya)
            at = pair ^ (y_high * 4 + z_high * 2 + (za ^ zb))
            start = pl.multiple_of(at * 32, 32)
            q_out[c, group * 32 : (group + 1) * 32, :] = q_all[pl.ds(start, 32), :]


def query_call(features, other, salt, mult, offs, thr):
    return call(
        query_kernel,
        [
            ((2, 256, 256), jnp.bfloat16),
            ((128, 128), jnp.int32),
            ((8, 128), jnp.float32),
        ],
        "hvvvvv",
        scratch=[
            pltpu.VMEM((256, 256), jnp.bfloat16),
            pltpu.VMEM((128, 256), jnp.bfloat16),
            pltpu.SemaphoreType.DMA,
        ],
        limit=8,
        flops=4_000_000,
    )(features, other, salt, mult, offs, thr)


def gram_kernel01(slot, part, own, other, q, salt, mult, offs, thr, own_sq, *outs):
    *blocks, sq_out, cols = outs
    fill(slot, part, own, other, q, salt, mult, offs, thr, own_sq, blocks, cols, sq_out, None)


def gram_kernel2(
    slot, part, own, other, q, salt, mult, offs, thr, own_sq, sq_query, sq0s, sq0k, sq1, *outs
):
    *blocks, cols, extra = outs
    more = (sq_query, sq0s, sq0k, sq1, extra)
    fill(slot, part, own, other, q, salt, mult, offs, thr, own_sq, blocks, cols, None, more)


def fill(slot, part, own, other, q, salt, mult, offs, thr, own_sq, blocks, cols, sq_out, more):
    lanes_of = SLOT_TILES[slot]
    n = len(lanes_of)
    send, keep = blocks[0], blocks[-1]
    core, _, tile = my_place()
    for here, i in enumerate(part):
        xa, c, xb = ORDER[i]
        base = tile_at(core, tile, c, xa, xb) * 16 + core * 8
        first = lanes_of[0] * 128
        cols[here, 0:128, :] = own[i, :, first : first + n * 128]
        for k, l in enumerate(lanes_of):
            m, o, t = (ref[block_row(base, l), :] for ref in (mult, offs, thr))
            lanes = slice(k * 128, (k + 1) * 128)
            x = other[here, :, lanes]
            total = jnp.sum(x * x, axis=0, keepdims=True) + own_sq[i, l : l + 1, :]
            if more is None:
                sq_out[here, k : k + 1, :] = total
            else:
                more[4][here, l : l + 1, :] = total
            cols[here, 128:256, lanes] = sample(x, salt[...], m, o, t, weight_of(t))
        if more is not None:
            sq0 = more[1] if i < 4 else more[2]
            more[4][here, 0:3, :] = sq0[i % 4, 0:3, :]
            more[4][here, 3:6, :] = more[3][i, 0:3, :]
        gram = jnp.dot(q[c], cols[here], preferred_element_type=jnp.float32)
        for group in range(8):
            ya, za, zb = group >> 2, group >> 1 & 1, group & 1
            near = (xa, ya, za)
            at = sum(near[(slot + k) % 3] << (5 - k) for k in range(1, 3))
            at += xb + (c ^ ya) * 2 + zb * 4
            ref = send if near[slot] else keep
            for k in range(n):
                ref[at, k * 32 : (k + 1) * 32, :] = gram[
                    group * 32 : (group + 1) * 32, k * 128 : (k + 1) * 128
                ]
            if more is not None:
                ref[at, 64:72, :] = more[4][here]
                ref[at, 72:80, :] = more[0][...]


def gram_call(slot, part, own, other, q, salt, mult, offs, thr, own_sq, *more):
    n = len(SLOT_TILES[slot])
    height = SLOT_ROWS[slot]
    count = 2 if len(part) == 8 else 1
    out_shape = [((32, height, 128), jnp.float32)] * count
    scratch = [pltpu.VMEM((len(part), 256, n * 128), jnp.bfloat16)]
    if slot == 2:
        kernel = gram_kernel2
        scratch.append(pltpu.VMEM((8, 8, 128), jnp.float32))
    else:
        kernel = gram_kernel01
        out_shape.append(((len(part), 8, 128), jnp.float32))
    return call(
        functools.partial(kernel, slot, part),
        out_shape,
        "v" * (8 + len(more)),
        scratch=scratch,
        flops=n * len(part) * 16_000_000,
        nbytes=5 << 20,
    )(own, other, q, salt, mult, offs, thr, own_sq, *more)


def join_kernel(*refs):
    outs = refs[6:]
    for j in range(8):
        row = 0
        for slot in range(3):
            height = SLOT_ROWS[slot]
            outs[j][row : row + height, :] = refs[slot][j] + refs[3 + slot][j]
            row += height


def join_call(keeps, gots):
    return call(
        join_kernel, [((ALL_ROWS, 128), jnp.float32)] * 8, "v" * 6, limit=8, nbytes=4 << 20
    )(*keeps, *gots)


def last_sum_kernel(*refs):
    send, keep = refs[8:]
    core, _, _ = my_place()

    def total(start, height):
        parts = [ref[start : start + height, :] for ref in refs[:8]]
        return ((parts[0] + parts[1]) + (parts[2] + parts[3])) + (
            (parts[4] + parts[5]) + (parts[6] + parts[7])
        )

    for l in range(8):
        start = l * 32
        even, odd = total(start, 16), total(start + 16, 16)
        keep[l * 16 : (l + 1) * 16, :] = jnp.where(core == 0, even, odd)
        send[l * 16 : (l + 1) * 16, :] = jnp.where(core == 0, odd, even)
    squares = total(256, 8)
    send[128:136, :] = squares
    keep[128:136, :] = squares
    keep[136:144, :] = total(264, 8)


def last_sum_call(parts):
    return call(
        last_sum_kernel, [((136, 128), jnp.float32), ((144, 128), jnp.float32)], "v" * 8, limit=4
    )(*parts)


def finish_kernel(keep, other, out):
    core, pair, _ = my_place()
    row = pair * 2 + core
    line = jnp.broadcast_to(keep[pl.ds(136 + row // 8, 1), :], (16, 128))
    lane = lax.broadcasted_iota(jnp.int32, (16, 128), 1)
    spot = lax.broadcasted_iota(jnp.int32, (16, 128), 0) + (row % 8) * 16
    squares = jnp.sum(jnp.where(lane == spot, line, 0.0), axis=1, keepdims=True)
    query_norm = jnp.sqrt(squares + 1e-06)
    for source, half in ((keep, core), (other, 1 - core)):
        for l in range(8):
            norm = jnp.sqrt(source[128 + l : 129 + l, :] + 1e-06)
            at = pl.multiple_of(half * 1024 + l * 128, 128)
            out[:, pl.ds(at, 128)] = source[l * 16 : (l + 1) * 16, :] / (query_norm * norm)


def finish_call(keep, other):
    return call(finish_kernel, [((16, 2048), jnp.float32)], "vv", limit=4)(keep, other)[0]


def permute(x, pairs):
    return lax.ppermute(x, AXES, pairs)


def body(features, row_salt, column_multiplier, column_offset, thresholds):
    salt = row_salt.reshape(1, 128)
    params = [a.reshape(128, 128) for a in (column_multiplier, column_offset, thresholds)]
    partner = [(i, i ^ 8) for i in range(128)]
    xq, x0s, x1, x2, x0k = cast_call(features, salt)
    yq = permute(xq, partner)
    y0s = permute(x0s, partner)
    y1 = permute(x1, partner)
    y2 = permute(x2, partner)
    y0k = permute(x0k, partner)
    own, own_sq = own_call(features, salt, *params)
    q, salts, sq_query = query_call(features, yq, salt, *params)

    def gram(slot, part, other, *more):
        return gram_call(slot, part, own, other, q, salts, *params, own_sq, *more)

    everything = range(8)
    send0, sq0s = gram(0, range(4), y0s)
    send1, keep1, sq1 = gram(1, everything, y1)
    keep0, sq0k = gram(0, range(4, 8), y0k)
    send2, keep2 = gram(2, everything, y2, sq_query, sq0s, sq0k, sq1)
    sends, keeps, gots = [send0, send1, send2], [keep0, keep1, keep2], [None] * 3
    none = [0, 0, 0]
    for step in range(3):
        half = 16 >> step
        for slot in range(3):
            got = permute(sends[slot], moves(axis_bits(slot + step), none))
            kept = keeps[slot]
            if step < 2:
                sends[slot] = kept[half:] + got[half:]
                keeps[slot] = kept[:half] + got[:half]
            else:
                gots[slot] = got
    chunks = join_call(keeps, gots)
    parts = [chunks[0]]
    for j in (7, 6, 5, 3, 4, 2, 1):
        parts.append(permute(chunks[j], moves(none, [j & 1, j >> 1 & 1, j >> 2])))
    send, keep = last_sum_call(parts)
    return finish_call(keep, permute(send, partner))


def solution(mesh):
    placed = (P(AXES, None), P(AXES), P(), P(), P())
    return jax.shard_map(
        body, mesh=mesh, in_specs=placed, out_specs=P("rows", "tiles"), check_vma=False
    )
```

time: 319 us -> 81.5 us (0.26)
  waiting for transfers between devices: 282 us -> 26 us
  starting transfers between devices: 0.09 us -> 43.2 us
  between operations: 14.9 us -> 0.13 us
  other arithmetic: 13.2 us -> 0.79 us
  Pallas kernels: 0 us -> 8.32 us
  matrix products: 8.08 us -> 0 us
    reduce_scatter x2 -> x0, waiting for transfers between devices: 174 us -> none  [the longest x1 174 us: shards(): lax.psum_scatter(partial_value, 'tiles', scatter_dimension=1, tiled=True)]
    psum x1 -> x0, waiting for transfers between devices: 107 us -> none  [shards(): squares = lax.psum(jnp.sum(wide * wide, axis=0), ('rows', 'tiles'))]
    ppermute x0 -> x22, starting transfers between devices: none -> 43.2 us  [permute(): return lax.ppermute(x, AXES, pairs)]
    ppermute x0 -> x22, waiting for transfers between devices: none -> 26 us  [permute(): return lax.ppermute(x, AXES, pairs)]
    reduce_sum x1 -> x0, other arithmetic: 9.86 us -> none  [shards(): squares = lax.psum(jnp.sum(wide * wide, axis=0), ('rows', 'tiles'))]
    pallas_call x0 -> x10, Pallas kernels: none -> 8.32 us  [the longest x4 3.77 us: gram_call(): call(functools.partial(kernel, slot, part), out_shape, 'v' * (8 + len(mor...]
    dot_general x1 -> x0, matrix products: 8.08 us -> none  [inner_product(): lax.dot_general(left, right, (((0,), (0,)), ((), ())), preferred_element_...]
  transfers between devices with their start and end apart: 3 -> 22, of which waited for: 2 -> 14; matrix products, arithmetic and copies ran while one was open for 0% -> 1% of each run, Pallas kernels for 0% -> 8%
where the time goes in v1:
time: 81.5 us; the launch traced here: 81.3 us
  starting transfers between devices  43.2 us (53%)
  waiting for transfers between devices  26 us (32%)
  Pallas kernels  8.32 us (10%)
  local copies, waits for them, and re-layouts  2.85 us (3%)
    ppermute x22, starting transfers between devices, permute(): return lax.ppermute(x, AXES, pairs)  43.2 us
    ppermute x22, waiting for transfers between devices, permute(): return lax.ppermute(x, AXES, pairs)  26 us
    pallas_call x4, Pallas kernels, gram_call(): call(functools.partial(kernel, slot, part), out_shape, 'v' * (8 + len(mor...  3.77 us
    unnamed x10, local copies, waits for them, and re-layouts  2.85 us
    pallas_call x1, Pallas kernels, own_call(): call(own_kernel, [((8, 128, 1024), jnp.bfloat16), ((8, 8, 128), jnp.float...  2.68 us
  transfers between devices with their start and end apart: 22, of which 14 were waited for; matrix products, arithmetic and copies ran while one was open for 1% of the time, Pallas kernels for 8%

profile of v1, /device:TPU:1, one launch (start us, length us, event | category | flops | bytes accessed | tf_op | source)
XLA Modules:
  0.0 81.3 jit_solution(4682899319774443371)
XLA Ops:
  0.0 2.2 %copy-done = bf16[128,16384]{1,0:T(8,128)(2,1)S(1)} copy-done((bf16[128,16384]{1,0:T(8,128)(2,1)S(1)}, bf16[128,16384]{1,0:T(8,128)(2,1)}, u32[]{:S(2)}) %copy-start) | copy-done | bytes 4194328
  2.2 0.7 copy-done.4
  2.9 0.6 shard_map.56
  3.4 1.5 %collective-permute-start.5 = (f32[8,128,384]{2,1,0:T(8,128)S(1)}, f32[8,128,384]{2,1,0:T(8,128)S(1)}, u32[]{:S(2)}, u32[]{:S(2)}) collective-permute-start(f32[8,128,384]{2,1,0:T(8,128)S(1)} %get-tuple-element.43), channel_id=1, source_target_pairs={{0,8},{1,9},{2,10},{3,11},{4,12},{5,13},{6,14},{7,15},{8,0},{9,1},... | collective-permute-start | bytes 4718600 | tf_op jit(solution)/shard_map/ppermute | solution.py:371
  4.9 0.1 collective-permute-start.2
  5.0 0.4 collective-permute-start.1
  5.4 0.1 collective-permute-start.8
  5.5 2.7 %shard_map.55 = (bf16[8,128,1024]{2,1,0:T(8,128)(2,1)S(1)}, f32[8,8,128]{2,1,0:T(8,128)S(1)}) custom-call(bf16[128,16384]{1,0:T(8,128)(2,1)S(1)} %copy-done, s32[1,128]{1,0:T(1,128)S(1)} %bitcast.23, s32[128,128]{1,0:T(8,128)S(1)} %bitcast.4, s32[128,128]{1,0:T(8,128)S(1)} %bitcast.10, s32[128,128]{1,0:T(8,128)S(1)} %bitcast.16), custom_call_target="tpu_custom_call" | custom-call | flops 20000000 | bytes 4194304 | tf_op jit(solution)/shard_map/pallas_call | solution.py:170
  8.2 1.1 %collective-permute-done.1.other = f32[136,256]{1,0:T(8,128)S(1)} collective-permute-done((f32[136,256]{1,0:T(8,128)S(1)}, f32[136,256]{1,0:T(8,128)S(1)}, u32[]{:S(2)}, u32[]{:S(2)}) %collective-permute-start.1) | collective-permute-done | bytes 139296 | tf_op jit(solution)/shard_map/ppermute | solution.py:371
  9.2 0.3 shard_map.57
  9.6 0.8 shard_map.59
  10.4 2.7 %collective-permute-start.3 = (f32[32,96,128]{2,1,0:T(8,128)S(1)}, f32[32,96,128]{2,1,0:T(8,128)S(1)}, u32[]{:S(2)}, u32[]{:S(2)}) collective-permute-start(f32[32,96,128]{2,1,0:T(8,128)S(1)} %get-tuple-element.42), channel_id=1, source_target_pairs={{0,1},{1,0},{2,3},{3,2},{4,5},{5,4},{6,7},{7,6},{8,11},{9,10},{10,... | collective-permute-start | bytes 4718600 | tf_op jit(solution)/shard_map/ppermute | solution.py:371
  13.0 1.3 %shard_map.60 = (f32[32,96,128]{2,1,0:T(8,128)S(1)}, f32[32,96,128]{2,1,0:T(8,128)S(1)}, f32[8,8,128]{2,1,0:T(8,128)S(1)}) custom-call(bf16[8,128,1024]{2,1,0:T(8,128)(2,1)S(1)} %get-tuple-element.34.own, f32[8,128,384]{2,1,0:T(8,128)S(1)} %collective-permute-done.5.other, bf16[2,256,256]{2,1,0:T(8,128)(2,1)S(1)} %get-tuple-element.37.q, ...), custom_call_target="tpu_custom_call" | custom-call | flops 384000000 | bytes 5242880 | tf_op jit(solution)/shard_map/pallas_call | solution.py:298
  14.4 2.8 %collective-permute-start.6 = (f32[32,96,128]{2,1,0:T(8,128)S(1)}, f32[32,96,128]{2,1,0:T(8,128)S(1)}, u32[]{:S(2)}, u32[]{:S(2)}) collective-permute-start(f32[32,96,128]{2,1,0:T(8,128)S(1)} %get-tuple-element.45), channel_id=1, source_target_pairs={{0,4},{1,5},{2,6},{3,7},{4,0},{5,1},{6,2},{7,3},{8,76},{9,77},{10,... | collective-permute-start | bytes 4718600 | tf_op jit(solution)/shard_map/ppermute | solution.py:371
  17.2 0.7 shard_map.58
  17.9 1.0 %shard_map.61 = (f32[32,80,128]{2,1,0:T(8,128)S(1)}, f32[32,80,128]{2,1,0:T(8,128)S(1)}) custom-call(bf16[8,128,1024]{2,1,0:T(8,128)(2,1)S(1)} %get-tuple-element.34.own, f32[8,128,256]{2,1,0:T(8,128)S(1)} %collective-permute-done.8.other, bf16[2,256,256]{2,1,0:T(8,128)(2,1)S(1)} %get-tuple-element.37.q, s32[128,128]{1,0:T(8,128)S(1)} %get-tuple-element.38.salt, ...), custom_call_target="tpu_custom_call" | custom-call | flops 256000000 | bytes 5242880 | tf_op jit(solution)/shard_map/pallas_call | solution.py:298
  18.9 3.8 %collective-permute-start.9 = (f32[32,80,128]{2,1,0:T(8,128)S(1)}, f32[32,80,128]{2,1,0:T(8,128)S(1)}, u32[]{:S(2)}, u32[]{:S(2)}) collective-permute-start(f32[32,80,128]{2,1,0:T(8,128)S(1)} %get-tuple-element.52), channel_id=1, source_target_pairs={{0,16},{1,17},{2,18},{3,19},{4,20},{5,21},{6,22},{7,23},{8,56},{9,... | collective-permute-start | bytes 3932168 | tf_op jit(solution)/shard_map/ppermute | solution.py:371
  22.7 8.2 %collective-permute-done.3 = f32[32,96,128]{2,1,0:T(8,128)S(1)} collective-permute-done((f32[32,96,128]{2,1,0:T(8,128)S(1)}, f32[32,96,128]{2,1,0:T(8,128)S(1)}, u32[]{:S(2)}, u32[]{:S(2)}) %collective-permute-start.3) | collective-permute-done | bytes 1572896 | tf_op jit(solution)/shard_map/ppermute | solution.py:371
  30.9 0.2 slice_add_fusion.3
  31.1 2.9 %collective-permute-start.4 = (f32[16,96,128]{2,1,0:T(8,128)S(1)}, f32[16,96,128]{2,1,0:T(8,128)S(1)}, u32[]{:S(2)}, u32[]{:S(2)}) collective-permute-start(f32[16,96,128]{2,1,0:T(8,128)S(1)} %get-tuple-element.66), channel_id=1, source_target_pairs={{0,4},{1,5},{2,6},{3,7},{4,0},{5,1},{6,2},{7,3},{8,76},{9,77},{10,... | collective-permute-start | bytes 2359304 | tf_op jit(solution)/shard_map/ppermute | solution.py:371
  34.1 0.9 %collective-permute-done.6 = f32[32,96,128]{2,1,0:T(8,128)S(1)} collective-permute-done((f32[32,96,128]{2,1,0:T(8,128)S(1)}, f32[32,96,128]{2,1,0:T(8,128)S(1)}, u32[]{:S(2)}, u32[]{:S(2)}) %collective-permute-start.6) | collective-permute-done | bytes 1572896 | tf_op jit(solution)/shard_map/ppermute | solution.py:371
  35.0 0.2 slice_add_fusion.1
  35.2 3.8 %collective-permute-start.7 = (f32[16,96,128]{2,1,0:T(8,128)S(1)}, f32[16,96,128]{2,1,0:T(8,128)S(1)}, u32[]{:S(2)}, u32[]{:S(2)}) collective-permute-start(f32[16,96,128]{2,1,0:T(8,128)S(1)} %get-tuple-element.64), channel_id=1, source_target_pairs={{0,16},{1,17},{2,18},{3,19},{4,20},{5,21},{6,22},{7,23},{8,56},{9,... | collective-permute-start | bytes 2359304 | tf_op jit(solution)/shard_map/ppermute | solution.py:371
  39.0 0.1 slice_add_fusion.5
  39.2 1.6 %collective-permute-start.10 = (f32[16,80,128]{2,1,0:T(8,128)S(1)}, f32[16,80,128]{2,1,0:T(8,128)S(1)}, u32[]{:S(2)}, u32[]{:S(2)}) collective-permute-start(f32[16,80,128]{2,1,0:T(8,128)S(1)} %get-tuple-element.68), channel_id=1, source_target_pairs={{0,1},{1,0},{2,3},{3,2},{4,5},{5,4},{6,7},{7,6},{8,11},{9,10},{10,... | collective-permute-start | bytes 1966088 | tf_op jit(solution)/shard_map/ppermute | solution.py:371
  40.8 2.6 %collective-permute-done.4 = f32[16,96,128]{2,1,0:T(8,128)S(1)} collective-permute-done((f32[16,96,128]{2,1,0:T(8,128)S(1)}, f32[16,96,128]{2,1,0:T(8,128)S(1)}, u32[]{:S(2)}, u32[]{:S(2)}) %collective-permute-start.4) | collective-permute-done | bytes 786464 | tf_op jit(solution)/shard_map/ppermute | solution.py:371
  43.4 0.1 slice_add_fusion.7
  43.5 3.8 %collective-permute-start.11 = (f32[8,96,128]{2,1,0:T(8,128)S(1)}, f32[8,96,128]{2,1,0:T(8,128)S(1)}, u32[]{:S(2)}, u32[]{:S(2)}) collective-permute-start(f32[8,96,128]{2,1,0:T(8,128)S(1)} %get-tuple-element.71), channel_id=1, source_target_pairs={{0,16},{1,17},{2,18},{3,19},{4,20},{5,21},{6,22},{7,23},{8,56},{9,... | collective-permute-start | bytes 1179656 | tf_op jit(solution)/shard_map/ppermute | solution.py:371
  47.4 1.0 %collective-permute-done.7 = f32[16,96,128]{2,1,0:T(8,128)S(1)} collective-permute-done((f32[16,96,128]{2,1,0:T(8,128)S(1)}, f32[16,96,128]{2,1,0:T(8,128)S(1)}, u32[]{:S(2)}, u32[]{:S(2)}) %collective-permute-start.7) | collective-permute-done | bytes 786464 | tf_op jit(solution)/shard_map/ppermute | solution.py:371
  48.4 0.1 slice_add_fusion.6
  48.5 1.6 %collective-permute-start.12 = (f32[8,96,128]{2,1,0:T(8,128)S(1)}, f32[8,96,128]{2,1,0:T(8,128)S(1)}, u32[]{:S(2)}, u32[]{:S(2)}) collective-permute-start(f32[8,96,128]{2,1,0:T(8,128)S(1)} %get-tuple-element.69), channel_id=1, source_target_pairs={{0,1},{1,0},{2,3},{3,2},{4,5},{5,4},{6,7},{7,6},{8,11},{9,10},{10,... | collective-permute-start | bytes 1179656 | tf_op jit(solution)/shard_map/ppermute | solution.py:371
  50.2 2.6 %collective-permute-start.13 = (f32[8,80,128]{2,1,0:T(8,128)S(1)}, f32[8,80,128]{2,1,0:T(8,128)S(1)}, u32[]{:S(2)}, u32[]{:S(2)}) collective-permute-start(f32[8,80,128]{2,1,0:T(8,128)S(1)} %get-tuple-element.73), channel_id=1, source_target_pairs={{0,4},{1,5},{2,6},{3,7},{4,0},{5,1},{6,2},{7,3},{8,76},{9,77},{10,... | collective-permute-start | bytes 983048 | tf_op jit(solution)/shard_map/ppermute | solution.py:371
  52.9 4.6 %collective-permute-done.13.refs_5_ = f32[8,80,128]{2,1,0:T(8,128)S(1)} collective-permute-done((f32[8,80,128]{2,1,0:T(8,128)S(1)}, f32[8,80,128]{2,1,0:T(8,128)S(1)}, u32[]{:S(2)}, u32[]{:S(2)}) %collective-permute-start.13) | collective-permute-done | bytes 327712 | tf_op jit(solution)/shard_map/ppermute | solution.py:371
  57.4 0.1 shard_map.62
  57.7 2.0 %collective-permute-start.15 = (f32[272,128]{1,0:T(8,128)S(1)}, f32[272,128]{1,0:T(8,128)S(1)}, u32[]{:S(2)}, u32[]{:S(2)}) collective-permute-start(f32[272,128]{1,0:T(8,128)S(1)} %get-tuple-element.55), channel_id=1, source_target_pairs={{0,116},{1,117},{2,118},{3,119},{4,112},{5,113},{6,114},{7,115},{8... | collective-permute-start | bytes 417800 | tf_op jit(solution)/shard_map/ppermute | solution.py:371
  59.7 0.8 %collective-permute-start.16 = (f32[272,128]{1,0:T(8,128)S(1)}, f32[272,128]{1,0:T(8,128)S(1)}, u32[]{:S(2)}, u32[]{:S(2)}) collective-permute-start(f32[272,128]{1,0:T(8,128)S(1)} %get-tuple-element.56), channel_id=1, source_target_pairs={{0,51},{1,50},{2,49},{3,48},{4,55},{5,54},{6,53},{7,52},{8,25},{9,... | collective-permute-start | bytes 417800 | tf_op jit(solution)/shard_map/ppermute | solution.py:371
  60.5 0.7 collective-permute-start.17
  61.3 1.1 %collective-permute-start.18 = (f32[272,128]{1,0:T(8,128)S(1)}, f32[272,128]{1,0:T(8,128)S(1)}, u32[]{:S(2)}, u32[]{:S(2)}) collective-permute-start(f32[272,128]{1,0:T(8,128)S(1)} %get-tuple-element.58), channel_id=1, source_target_pairs={{0,48},{1,49},{2,50},{3,51},{4,52},{5,53},{6,54},{7,55},{8,24},{9,... | collective-permute-start | bytes 417800 | tf_op jit(solution)/shard_map/ppermute | solution.py:371
  62.4 1.5 %collective-permute-done.14.refs_1_ = f32[272,128]{1,0:T(8,128)S(1)} collective-permute-done((f32[272,128]{1,0:T(8,128)S(1)}, f32[272,128]{1,0:T(8,128)S(1)}, u32[]{:S(2)}, u32[]{:S(2)}) %collective-permute-start.14) | collective-permute-done | bytes 139296 | tf_op jit(solution)/shard_map/ppermute | solution.py:371
  63.9 1.3 %collective-permute-done.15.refs_2_ = f32[272,128]{1,0:T(8,128)S(1)} collective-permute-done((f32[272,128]{1,0:T(8,128)S(1)}, f32[272,128]{1,0:T(8,128)S(1)}, u32[]{:S(2)}, u32[]{:S(2)}) %collective-permute-start.15) | collective-permute-done | bytes 139296 | tf_op jit(solution)/shard_map/ppermute | solution.py:371
  65.1 0.5 collective-permute-done.16.refs_3_
  65.6 0.4 collective-permute-done.17.refs_4_
  66.0 1.0 %collective-permute-done.18.refs_5_ = f32[272,128]{1,0:T(8,128)S(1)} collective-permute-done((f32[272,128]{1,0:T(8,128)S(1)}, f32[272,128]{1,0:T(8,128)S(1)}, u32[]{:S(2)}, u32[]{:S(2)}) %collective-permute-start.18) | collective-permute-done | bytes 139296 | tf_op jit(solution)/shard_map/ppermute | solution.py:371
  67.0 0.8 collective-permute-done.19.refs_6_
  67.8 1.3 %collective-permute-done.20.refs_7_ = f32[272,128]{1,0:T(8,128)S(1)} collective-permute-done((f32[272,128]{1,0:T(8,128)S(1)}, f32[272,128]{1,0:T(8,128)S(1)}, u32[]{:S(2)}, u32[]{:S(2)}) %collective-permute-start.20) | collective-permute-done | bytes 139296 | tf_op jit(solution)/shard_map/ppermute | solution.py:371
  69.1 10.5 %collective-permute-start.21 = (f32[136,128]{1,0:T(8,128)S(1)}, f32[136,128]{1,0:T(8,128)S(1)}, u32[]{:S(2)}, u32[]{:S(2)}) collective-permute-start(f32[136,128]{1,0:T(8,128)S(1)} %get-tuple-element.62), channel_id=1, source_target_pairs={{0,8},{1,9},{2,10},{3,11},{4,12},{5,13},{6,14},{7,15},{8,0},{9,1},... | collective-permute-start | bytes 208904 | tf_op jit(solution)/shard_map/ppermute | solution.py:371
  79.7 0.9 %collective-permute-done.21.other = f32[136,128]{1,0:T(8,128)S(1)} collective-permute-done((f32[136,128]{1,0:T(8,128)S(1)}, f32[136,128]{1,0:T(8,128)S(1)}, u32[]{:S(2)}, u32[]{:S(2)}) %collective-permute-start.21) | collective-permute-done | bytes 69664 | tf_op jit(solution)/shard_map/ppermute | solution.py:371
  80.6 0.8 shard_map.64
  (22 shorter events, 0.3 us)
Async XLA Ops:
  0.0 2.2 %copy-start = (bf16[128,16384]{1,0:T(8,128)(2,1)S(1)}, bf16[128,16384]{1,0:T(8,128)(2,1)}, u32[]{:S(2)}) copy-start(bf16[128,16384]{1,0:T(8,128)(2,1)} %feat.5) | copy-start | bytes 12582916
  2.2 0.7 copy-start.4
  2.8 2.6 %copy-start.1 = (s32[16384]{0:T(1024)S(1)}, s32[16384]{0:T(1024)}, u32[]{:S(2)}) copy-start(s32[16384]{0:T(1024)} %param.7) | copy-start | bytes 196612
  2.8 2.6 %copy-start.2 = (s32[16384]{0:T(1024)S(1)}, s32[16384]{0:T(1024)}, u32[]{:S(2)}) copy-start(s32[16384]{0:T(1024)} %param.8) | copy-start | bytes 196612
  2.8 2.6 %copy-start.3 = (s32[16384]{0:T(1024)S(1)}, s32[16384]{0:T(1024)}, u32[]{:S(2)}) copy-start(s32[16384]{0:T(1024)} %param.9) | copy-start | bytes 196612
  3.4 9.6 %collective-permute-start.5 = (f32[8,128,384]{2,1,0:T(8,128)S(1)}, f32[8,128,384]{2,1,0:T(8,128)S(1)}, u32[]{:S(2)}, u32[]{:S(2)}) collective-permute-start(f32[8,128,384]{2,1,0:T(8,128)S(1)} %get-tuple-element.43), channel_id=1, source_target_pairs={{0,8},{1,9},{2,10},{3,11},{4,12},{5,13},{6,14},{7,15},{8,0},{9,1},... | collective-permute-start | bytes 4718600 | tf_op jit(solution)/shard_map/ppermute | solution.py:371
  4.9 4.7 %collective-permute-start.2 = (f32[4,128,384]{2,1,0:T(8,128)S(1)}, f32[4,128,384]{2,1,0:T(8,128)S(1)}, u32[]{:S(2)}, u32[]{:S(2)}) collective-permute-start(f32[4,128,384]{2,1,0:T(8,128)S(1)} %get-tuple-element.41), channel_id=1, source_target_pairs={{0,8},{1,9},{2,10},{3,11},{4,12},{5,13},{6,14},{7,15},{8,0},{9,1},... | collective-permute-start | bytes 2359304 | tf_op jit(solution)/shard_map/ppermute | solution.py:371
  5.0 4.3 %collective-permute-start.1 = (f32[136,256]{1,0:T(8,128)S(1)}, f32[136,256]{1,0:T(8,128)S(1)}, u32[]{:S(2)}, u32[]{:S(2)}) collective-permute-start(f32[136,256]{1,0:T(8,128)S(1)} %get-tuple-element.36), channel_id=1, source_target_pairs={{0,8},{1,9},{2,10},{3,11},{4,12},{5,13},{6,14},{7,15},{8,0},{9,1},... | collective-permute-start | bytes 417800 | tf_op jit(solution)/shard_map/ppermute | solution.py:371
  5.4 12.5 %collective-permute-start.8 = (f32[8,128,256]{2,1,0:T(8,128)S(1)}, f32[8,128,256]{2,1,0:T(8,128)S(1)}, u32[]{:S(2)}, u32[]{:S(2)}) collective-permute-start(f32[8,128,256]{2,1,0:T(8,128)S(1)} %get-tuple-element.46), channel_id=1, source_target_pairs={{0,8},{1,9},{2,10},{3,11},{4,12},{5,13},{6,14},{7,15},{8,0},{9,1},... | collective-permute-start | bytes 3145736 | tf_op jit(solution)/shard_map/ppermute | solution.py:371
  10.4 20.6 %collective-permute-start.3 = (f32[32,96,128]{2,1,0:T(8,128)S(1)}, f32[32,96,128]{2,1,0:T(8,128)S(1)}, u32[]{:S(2)}, u32[]{:S(2)}) collective-permute-start(f32[32,96,128]{2,1,0:T(8,128)S(1)} %get-tuple-element.42), channel_id=1, source_target_pairs={{0,1},{1,0},{2,3},{3,2},{4,5},{5,4},{6,7},{7,6},{8,11},{9,10},{10,... | collective-permute-start | bytes 4718600 | tf_op jit(solution)/shard_map/ppermute | solution.py:371
  13.0 4.1 %collective-permute-start = (f32[4,128,384]{2,1,0:T(8,128)S(1)}, f32[4,128,384]{2,1,0:T(8,128)S(1)}, u32[]{:S(2)}, u32[]{:S(2)}) collective-permute-start(f32[4,128,384]{2,1,0:T(8,128)S(1)} %get-tuple-element.35), channel_id=1, source_target_pairs={{0,8},{1,9},{2,10},{3,11},{4,12},{5,13},{6,14},{7,15},{8,0},{9,1},... | collective-permute-start | bytes 2359304 | tf_op jit(solution)/shard_map/ppermute | solution.py:371
  14.4 20.6 %collective-permute-start.6 = (f32[32,96,128]{2,1,0:T(8,128)S(1)}, f32[32,96,128]{2,1,0:T(8,128)S(1)}, u32[]{:S(2)}, u32[]{:S(2)}) collective-permute-start(f32[32,96,128]{2,1,0:T(8,128)S(1)} %get-tuple-element.45), channel_id=1, source_target_pairs={{0,4},{1,5},{2,6},{3,7},{4,0},{5,1},{6,2},{7,3},{8,76},{9,77},{10,... | collective-permute-start | bytes 4718600 | tf_op jit(solution)/shard_map/ppermute | solution.py:371
  18.9 20.1 %collective-permute-start.9 = (f32[32,80,128]{2,1,0:T(8,128)S(1)}, f32[32,80,128]{2,1,0:T(8,128)S(1)}, u32[]{:S(2)}, u32[]{:S(2)}) collective-permute-start(f32[32,80,128]{2,1,0:T(8,128)S(1)} %get-tuple-element.52), channel_id=1, source_target_pairs={{0,16},{1,17},{2,18},{3,19},{4,20},{5,21},{6,22},{7,23},{8,56},{9,... | collective-permute-start | bytes 3932168 | tf_op jit(solution)/shard_map/ppermute | solution.py:371
  31.1 12.3 %collective-permute-start.4 = (f32[16,96,128]{2,1,0:T(8,128)S(1)}, f32[16,96,128]{2,1,0:T(8,128)S(1)}, u32[]{:S(2)}, u32[]{:S(2)}) collective-permute-start(f32[16,96,128]{2,1,0:T(8,128)S(1)} %get-tuple-element.66), channel_id=1, source_target_pairs={{0,4},{1,5},{2,6},{3,7},{4,0},{5,1},{6,2},{7,3},{8,76},{9,77},{10,... | collective-permute-start | bytes 2359304 | tf_op jit(solution)/shard_map/ppermute | solution.py:371
  35.2 13.2 %collective-permute-start.7 = (f32[16,96,128]{2,1,0:T(8,128)S(1)}, f32[16,96,128]{2,1,0:T(8,128)S(1)}, u32[]{:S(2)}, u32[]{:S(2)}) collective-permute-start(f32[16,96,128]{2,1,0:T(8,128)S(1)} %get-tuple-element.64), channel_id=1, source_target_pairs={{0,16},{1,17},{2,18},{3,19},{4,20},{5,21},{6,22},{7,23},{8,56},{9,... | collective-permute-start | bytes 2359304 | tf_op jit(solution)/shard_map/ppermute | solution.py:371
  39.2 11.0 %collective-permute-start.10 = (f32[16,80,128]{2,1,0:T(8,128)S(1)}, f32[16,80,128]{2,1,0:T(8,128)S(1)}, u32[]{:S(2)}, u32[]{:S(2)}) collective-permute-start(f32[16,80,128]{2,1,0:T(8,128)S(1)} %get-tuple-element.68), channel_id=1, source_target_pairs={{0,1},{1,0},{2,3},{3,2},{4,5},{5,4},{6,7},{7,6},{8,11},{9,10},{10,... | collective-permute-start | bytes 1966088 | tf_op jit(solution)/shard_map/ppermute | solution.py:371
  43.5 9.3 %collective-permute-start.11 = (f32[8,96,128]{2,1,0:T(8,128)S(1)}, f32[8,96,128]{2,1,0:T(8,128)S(1)}, u32[]{:S(2)}, u32[]{:S(2)}) collective-permute-start(f32[8,96,128]{2,1,0:T(8,128)S(1)} %get-tuple-element.71), channel_id=1, source_target_pairs={{0,16},{1,17},{2,18},{3,19},{4,20},{5,21},{6,22},{7,23},{8,56},{9,... | collective-permute-start | bytes 1179656 | tf_op jit(solution)/shard_map/ppermute | solution.py:371
  48.5 8.9 %collective-permute-start.12 = (f32[8,96,128]{2,1,0:T(8,128)S(1)}, f32[8,96,128]{2,1,0:T(8,128)S(1)}, u32[]{:S(2)}, u32[]{:S(2)}) collective-permute-start(f32[8,96,128]{2,1,0:T(8,128)S(1)} %get-tuple-element.69), channel_id=1, source_target_pairs={{0,1},{1,0},{2,3},{3,2},{4,5},{5,4},{6,7},{7,6},{8,11},{9,10},{10,... | collective-permute-start | bytes 1179656 | tf_op jit(solution)/shard_map/ppermute | solution.py:371
  50.2 7.2 %collective-permute-start.13 = (f32[8,80,128]{2,1,0:T(8,128)S(1)}, f32[8,80,128]{2,1,0:T(8,128)S(1)}, u32[]{:S(2)}, u32[]{:S(2)}) collective-permute-start(f32[8,80,128]{2,1,0:T(8,128)S(1)} %get-tuple-element.73), channel_id=1, source_target_pairs={{0,4},{1,5},{2,6},{3,7},{4,0},{5,1},{6,2},{7,3},{8,76},{9,77},{10,... | collective-permute-start | bytes 983048 | tf_op jit(solution)/shard_map/ppermute | solution.py:371
  57.6 6.3 %collective-permute-start.14 = (f32[272,128]{1,0:T(8,128)S(1)}, f32[272,128]{1,0:T(8,128)S(1)}, u32[]{:S(2)}, u32[]{:S(2)}) collective-permute-start(f32[272,128]{1,0:T(8,128)S(1)} %get-tuple-element.54), channel_id=1, source_target_pairs={{0,119},{1,118},{2,117},{3,116},{4,115},{5,114},{6,113},{7,112},{8... | collective-permute-start | bytes 417800 | tf_op jit(solution)/shard_map/ppermute | solution.py:371
  57.7 7.5 %collective-permute-start.15 = (f32[272,128]{1,0:T(8,128)S(1)}, f32[272,128]{1,0:T(8,128)S(1)}, u32[]{:S(2)}, u32[]{:S(2)}) collective-permute-start(f32[272,128]{1,0:T(8,128)S(1)} %get-tuple-element.55), channel_id=1, source_target_pairs={{0,116},{1,117},{2,118},{3,119},{4,112},{5,113},{6,114},{7,115},{8... | collective-permute-start | bytes 417800 | tf_op jit(solution)/shard_map/ppermute | solution.py:371
  59.7 5.9 %collective-permute-start.16 = (f32[272,128]{1,0:T(8,128)S(1)}, f32[272,128]{1,0:T(8,128)S(1)}, u32[]{:S(2)}, u32[]{:S(2)}) collective-permute-start(f32[272,128]{1,0:T(8,128)S(1)} %get-tuple-element.56), channel_id=1, source_target_pairs={{0,51},{1,50},{2,49},{3,48},{4,55},{5,54},{6,53},{7,52},{8,25},{9,... | collective-permute-start | bytes 417800 | tf_op jit(solution)/shard_map/ppermute | solution.py:371
  60.5 5.5 %collective-permute-start.17 = (f32[272,128]{1,0:T(8,128)S(1)}, f32[272,128]{1,0:T(8,128)S(1)}, u32[]{:S(2)}, u32[]{:S(2)}) collective-permute-start(f32[272,128]{1,0:T(8,128)S(1)} %get-tuple-element.57), channel_id=1, source_target_pairs={{0,71},{1,70},{2,69},{3,68},{4,67},{5,66},{6,65},{7,64},{8,13},{9,... | collective-permute-start | bytes 417800 | tf_op jit(solution)/shard_map/ppermute | solution.py:371
  61.3 5.7 %collective-permute-start.18 = (f32[272,128]{1,0:T(8,128)S(1)}, f32[272,128]{1,0:T(8,128)S(1)}, u32[]{:S(2)}, u32[]{:S(2)}) collective-permute-start(f32[272,128]{1,0:T(8,128)S(1)} %get-tuple-element.58), channel_id=1, source_target_pairs={{0,48},{1,49},{2,50},{3,51},{4,52},{5,53},{6,54},{7,55},{8,24},{9,... | collective-permute-start | bytes 417800 | tf_op jit(solution)/shard_map/ppermute | solution.py:371
  63.9 3.9 %collective-permute-start.19 = (f32[272,128]{1,0:T(8,128)S(1)}, f32[272,128]{1,0:T(8,128)S(1)}, u32[]{:S(2)}, u32[]{:S(2)}) collective-permute-start(f32[272,128]{1,0:T(8,128)S(1)} %get-tuple-element.59), channel_id=1, source_target_pairs={{0,68},{1,69},{2,70},{3,71},{4,64},{5,65},{6,66},{7,67},{8,12},{9,... | collective-permute-start | bytes 417800 | tf_op jit(solution)/shard_map/ppermute | solution.py:371
  65.1 3.9 %collective-permute-start.20 = (f32[272,128]{1,0:T(8,128)S(1)}, f32[272,128]{1,0:T(8,128)S(1)}, u32[]{:S(2)}, u32[]{:S(2)}) collective-permute-start(f32[272,128]{1,0:T(8,128)S(1)} %get-tuple-element.60), channel_id=1, source_target_pairs={{0,3},{1,2},{2,1},{3,0},{4,7},{5,6},{6,5},{7,4},{8,9},{9,8},{10,11... | collective-permute-start | bytes 417800 | tf_op jit(solution)/shard_map/ppermute | solution.py:371
  69.1 11.4 %collective-permute-start.21 = (f32[136,128]{1,0:T(8,128)S(1)}, f32[136,128]{1,0:T(8,128)S(1)}, u32[]{:S(2)}, u32[]{:S(2)}) collective-permute-start(f32[136,128]{1,0:T(8,128)S(1)} %get-tuple-element.62), channel_id=1, source_target_pairs={{0,8},{1,9},{2,10},{3,11},{4,12},{5,13},{6,14},{7,15},{8,0},{9,1},... | collective-permute-start | bytes 208904 | tf_op jit(solution)/shard_map/ppermute | solution.py:371

commit v2 on v1

v2 whole, which is shorter than its diff:
```python
import functools

import jax
import jax.numpy as jnp
from jax import lax
from jax.experimental import pallas as pl
from jax.experimental.pallas import tpu as pltpu
from jax.sharding import PartitionSpec as P

AXES = ("rows", "tiles")
PRIME = 65521
SLOT_TILES = ((0, 1, 2), (3, 4, 5), (6, 7))
SLOT_ROWS = (96, 96, 80)


def place(index):
    rows, tiles = divmod(index, 8)
    return [tiles & 3, (rows >> 3) * 2 + (tiles >> 2), (rows >> 1) & 3], rows & 1


def index_of(chip, core):
    x, y, z = chip
    return (((y >> 1) << 3) | (z << 1) | core) * 8 + ((y & 1) << 2 | x)


def gray(v):
    return v ^ (v >> 1)


def flip(index, first, last):
    chip, core = place(index)
    for axis in range(3):
        mask = first[axis] << core | last[axis] << (1 - core)
        chip[axis] = gray(gray(chip[axis]) ^ mask)
    return index_of(chip, core)


def moves(first, last):
    return [(i, flip(i, first, last)) for i in range(128)]


def axis_bits(axis):
    return [int(a == axis % 3) for a in range(3)]


def my_place():
    rows = lax.axis_index("rows")
    tile = lax.axis_index("tiles")
    return rows & 1, rows >> 1, tile


def tile_at(core, tile, c, xa, xb):
    high = jnp.where(core == 0, xb, xa)
    return tile ^ (c * 4 + high * 2 + (xa ^ xb))


def weight_of(threshold):
    return lax.rsqrt(threshold.astype(jnp.float32) / 65521.0)


def fold(v):
    return v - (v >> 16) * PRIME


def sample(values, salt, multiplier, offset, threshold, weight):
    residue = fold(fold(salt * multiplier + offset))
    keep = (residue < threshold) | (residue >= PRIME)
    return jnp.where(keep, values * weight, 0.0).astype(jnp.bfloat16)


def call(kernel, out_shape, in_spaces, scratch=(), limit=16, flops=1_000_000, nbytes=1 << 20):
    spaces = {"v": pltpu.VMEM, "h": pltpu.HBM}
    return pl.pallas_call(
        kernel,
        out_shape=[jax.ShapeDtypeStruct(s, d) for s, d in out_shape],
        in_specs=[pl.BlockSpec(memory_space=spaces[s]) for s in in_spaces],
        out_specs=[pl.BlockSpec(memory_space=pltpu.VMEM)] * len(out_shape),
        scratch_shapes=list(scratch),
        compiler_params=pltpu.CompilerParams(vmem_limit_bytes=limit << 20),
        cost_estimate=pl.CostEstimate(flops=flops, bytes_accessed=nbytes, transcendentals=0),
    )


ORDER = [(xa, c, xb) for xa in (1, 0) for c in (0, 1) for xb in (0, 1)]


def cast_kernel(feat, outq, out0s, out1, out2, out0k, mine, queries, block, sems):
    core, _, tile = my_place()
    copies = [pltpu.make_async_copy(feat.at[:, 0:256], queries, sems.at[16])]
    for to, half, first in ((block, 1 - core, 0), (mine, core, 8)):
        for i, (xa, c, xb) in enumerate(ORDER):
            start = pl.multiple_of(tile_at(half, tile, c, xa, xb) * 2048 + half * 1024, 1024)
            copies.append(
                pltpu.make_async_copy(feat.at[:, pl.ds(start, 1024)], to.at[i], sems.at[first + i])
            )
    for copy in copies:
        copy.start()
    copies[0].wait()
    outq[...] = queries[...].astype(jnp.float32)
    for i in range(8):
        copies[1 + i].wait()
        out0 = out0s if i < 4 else out0k
        out0[i % 4] = block[i, :, 0:384].astype(jnp.float32)
        out1[i] = block[i, :, 384:768].astype(jnp.float32)
        out2[i] = block[i, :, 768:1024].astype(jnp.float32)
    for i in range(8):
        copies[9 + i].wait()


def cast_call(features):
    f32 = jnp.float32
    return call(
        cast_kernel,
        [
            ((128, 256), f32),
            ((4, 128, 384), f32),
            ((8, 128, 384), f32),
            ((8, 128, 256), f32),
            ((4, 128, 384), f32),
            ((8, 128, 1024), jnp.bfloat16),
            ((128, 256), jnp.bfloat16),
        ],
        "h",
        scratch=[
            pltpu.VMEM((8, 128, 1024), jnp.bfloat16),
            pltpu.SemaphoreType.DMA((17,)),
        ],
        limit=45,
        nbytes=6 << 20,
    )(features)


def column_of(row):
    return jnp.transpose(jnp.broadcast_to(row, (128, 128)))


def block_row(base, l):
    return pl.ds(base + l, 1)


def own_some(mine, salt, params, squares, places):
    core, _, tile = my_place()
    salts = column_of(salt[...])
    for i, at, outs in places:
        xa, c, xb = ORDER[i]
        base = tile_at(core, tile, c, xa, xb) * 16 + core * 8
        for slot, out, where in outs:
            for k, l in enumerate(SLOT_TILES[slot]):
                m, o, t = (ref[block_row(base, l), :] for ref in params)
                x = mine[i, :, l * 128 : (l + 1) * 128].astype(jnp.float32)
                squares[at, l : l + 1, :] = jnp.sum(x * x, axis=0, keepdims=True)
                out[where, :, k * 128 : (k + 1) * 128] = sample(x, salts, m, o, t, weight_of(t))


def own0s_kernel(mine, salt, mult, offs, thr, out0s, squares):
    places = [(i, i, [(0, out0s, i)]) for i in range(4)]
    own_some(mine, salt, (mult, offs, thr), squares, places)


def own_rest_kernel(mine, salt, mult, offs, thr, out1, out2, out0k, squares):
    places = []
    for i in range(8):
        outs = [(1, out1, i), (2, out2, i)]
        if i >= 4:
            outs.append((0, out0k, i - 4))
        places.append((i, i, outs))
    own_some(mine, salt, (mult, offs, thr), squares, places)


def own0s_call(mine, salt, mult, offs, thr):
    return call(
        own0s_kernel,
        [((4, 128, 384), jnp.bfloat16), ((4, 8, 128), jnp.float32)],
        "vvvvv",
        limit=8,
        flops=4_000_000,
        nbytes=1 << 20,
    )(mine, salt, mult, offs, thr)


def own_rest_call(mine, salt, mult, offs, thr):
    return call(
        own_rest_kernel,
        [
            ((8, 128, 384), jnp.bfloat16),
            ((8, 128, 256), jnp.bfloat16),
            ((4, 128, 384), jnp.bfloat16),
            ((8, 8, 128), jnp.float32),
        ],
        "vvvvv",
        limit=8,
        flops=16_000_000,
        nbytes=4 << 20,
    )(mine, salt, mult, offs, thr)


def query_kernel(
    queries, other, salt, other_salt, mult, offs, thr, q_out, salt_out, sq_out, q_all
):
    core, pair, _ = my_place()
    salts = (column_of(salt[...]), column_of(other_salt[...]))
    salt_out[...] = salts[1]
    sq_out[...] = jnp.zeros_like(sq_out)
    for l in range(2):
        lanes = slice(l * 128, (l + 1) * 128)
        m, o, t = (ref[l : l + 1, :] for ref in (mult, offs, thr))
        w = weight_of(t)
        total = None
        for u in range(2):
            source = queries if u == 0 else other
            x = source[:, lanes].astype(jnp.float32)
            part = jnp.sum(x * x, axis=0, keepdims=True)
            total = part if total is None else total + part
            value = sample(x, salts[u], m, o, t, w).astype(jnp.float32)
            q_all[lanes, u * 128 : (u + 1) * 128] = jnp.transpose(value).astype(jnp.bfloat16)
        sq_out[l : l + 1, :] = total
    for c in range(2):
        for group in range(8):
            ya, za, zb = group >> 2, group >> 1 & 1, group & 1
            z_high = jnp.where(core == 0, zb, za)
            y_high = jnp.where(core == 0, c ^ ya, ya)
            at = pair ^ (y_high * 4 + z_high * 2 + (za ^ zb))
            start = pl.multiple_of(at * 32, 32)
            q_out[c, group * 32 : (group + 1) * 32, :] = q_all[pl.ds(start, 32), :]


def query_call(queries, other, salt, other_salt, mult, offs, thr):
    return call(
        query_kernel,
        [
            ((2, 256, 256), jnp.bfloat16),
            ((128, 128), jnp.int32),
            ((8, 128), jnp.float32),
        ],
        "vvvvvvv",
        scratch=[pltpu.VMEM((256, 256), jnp.bfloat16)],
        limit=8,
        flops=4_000_000,
    )(queries, other, salt, other_salt, mult, offs, thr)


def gram_kernel01(slot, part, own, other, q, salt, mult, offs, thr, own_sq, *outs):
    *blocks, sq_out, cols = outs
    fill(slot, part, own, other, q, salt, (mult, offs, thr), own_sq, blocks, cols, sq_out, None)


def gram_kernel2(
    slot, part, own, other, q, salt, mult, offs, thr, own_sq, sq_query, sq0s, other0k, sq1, *outs
):
    *blocks, cols, extra = outs
    more = (sq_query, sq0s, other0k, sq1, extra)
    fill(slot, part, own, other, q, salt, (mult, offs, thr), own_sq, blocks, cols, None, more)


def sum_squares(x):
    return jnp.sum(x * x, axis=0, keepdims=True)


def fill(slot, part, own, other, q, salt, params, own_sq, blocks, cols, sq_out, more):
    lanes_of = SLOT_TILES[slot]
    n = len(lanes_of)
    send, keep = blocks[0], blocks[-1]
    core, _, tile = my_place()
    for here, i in enumerate(part):
        xa, c, xb = ORDER[i]
        base = tile_at(core, tile, c, xa, xb) * 16 + core * 8
        cols[here, 0:128, :] = own[here]
        for k, l in enumerate(lanes_of):
            m, o, t = (ref[block_row(base, l), :] for ref in params)
            lanes = slice(k * 128, (k + 1) * 128)
            x = other[here, :, lanes]
            if more is not None:
                more[4][here, l : l + 1, :] = sum_squares(x) + own_sq[i, l : l + 1, :]
            elif sq_out is not None:
                sq_out[here, k : k + 1, :] = sum_squares(x) + own_sq[i, l : l + 1, :]
            cols[here, 128:256, lanes] = sample(x, salt[...], m, o, t, weight_of(t))
        if more is not None:
            for l in range(3):
                if i < 4:
                    row = more[1][i, l : l + 1, :]
                else:
                    row = sum_squares(more[2][i - 4, :, l * 128 : (l + 1) * 128])
                    row = row + own_sq[i, l : l + 1, :]
                more[4][here, l : l + 1, :] = row
            more[4][here, 3:6, :] = more[3][i, 0:3, :]
        gram = jnp.dot(q[c], cols[here], preferred_element_type=jnp.float32)
        for group in range(8):
            ya, za, zb = group >> 2, group >> 1 & 1, group & 1
            near = (xa, ya, za)
            far = (xb, c ^ ya, zb)
            at = sum(near[(slot + k) % 3] << (5 - k) for k in range(1, 3))
            at += sum(far[(slot + k) % 3] << (2 - k) for k in range(3))
            ref = send if near[slot] else keep
            for k in range(n):
                ref[at, k * 32 : (k + 1) * 32, :] = gram[
                    group * 32 : (group + 1) * 32, k * 128 : (k + 1) * 128
                ]
            if more is not None:
                ref[at, 64:72, :] = more[4][here]
                ref[at, 72:80, :] = more[0][...]


def gram_call(slot, part, own, other, q, salt, mult, offs, thr, own_sq, *more):
    n = len(SLOT_TILES[slot])
    height = SLOT_ROWS[slot]
    count = 2 if len(part) == 8 else 1
    out_shape = [((32, height, 128), jnp.float32)] * count
    scratch = [pltpu.VMEM((len(part), 256, n * 128), jnp.bfloat16)]
    if slot == 2:
        kernel = gram_kernel2
        scratch.append(pltpu.VMEM((8, 8, 128), jnp.float32))
    else:
        kernel = gram_kernel01
        out_shape.append(((len(part), 8, 128), jnp.float32))
    return call(
        functools.partial(kernel, slot, part),
        out_shape,
        "v" * (8 + len(more)),
        scratch=scratch,
        flops=n * len(part) * 16_000_000,
        nbytes=5 << 20,
    )(own, other, q, salt, mult, offs, thr, own_sq, *more)


def last_sum_kernel(keep0, keep1, keep2, got0, got1, got2, send, keep):
    core, _, _ = my_place()
    slots = ((keep0, got0), (keep1, got1), (keep2, got2))

    def total(slot, start, height):
        rows = slice(start, start + height)
        return slots[slot][0][0, rows, :] + slots[slot][1][0, rows, :]

    for slot in range(3):
        for k, l in enumerate(SLOT_TILES[slot]):
            even, odd = total(slot, k * 32, 16), total(slot, k * 32 + 16, 16)
            keep[l * 16 : (l + 1) * 16, :] = jnp.where(core == 0, even, odd)
            send[l * 16 : (l + 1) * 16, :] = jnp.where(core == 0, odd, even)
    squares = total(2, 64, 8)
    send[128:136, :] = squares
    keep[128:136, :] = squares
    keep[136:144, :] = total(2, 72, 8)


def last_sum_call(keeps, gots):
    return call(
        last_sum_kernel, [((136, 128), jnp.float32), ((144, 128), jnp.float32)], "v" * 6, limit=4
    )(*keeps, *gots)


def finish_kernel(keep, other, out):
    core, pair, _ = my_place()
    row = pair * 2 + core
    line = jnp.broadcast_to(keep[pl.ds(136 + row // 8, 1), :], (16, 128))
    lane = lax.broadcasted_iota(jnp.int32, (16, 128), 1)
    spot = lax.broadcasted_iota(jnp.int32, (16, 128), 0) + (row % 8) * 16
    squares = jnp.sum(jnp.where(lane == spot, line, 0.0), axis=1, keepdims=True)
    query_norm = jnp.sqrt(squares + 1e-06)
    for source, half in ((keep, core), (other, 1 - core)):
        for l in range(8):
            norm = jnp.sqrt(source[128 + l : 129 + l, :] + 1e-06)
            at = pl.multiple_of(half * 1024 + l * 128, 128)
            out[:, pl.ds(at, 128)] = source[l * 16 : (l + 1) * 16, :] / (query_norm * norm)


def finish_call(keep, other):
    return call(finish_kernel, [((16, 2048), jnp.float32)], "vv", limit=4)(keep, other)[0]


def permute(x, pairs):
    return lax.ppermute(x, AXES, pairs)


def body(features, row_salt, column_multiplier, column_offset, thresholds):
    salt = row_salt.reshape(1, 128)
    params = [a.reshape(128, 128) for a in (column_multiplier, column_offset, thresholds)]
    partner = [(i, i ^ 8) for i in range(128)]
    other_salt = permute(salt, partner)
    xq, x0s, x1, x2, x0k, mine, queries = cast_call(features)
    yq = permute(xq, partner)
    y0s = permute(x0s, partner)
    y1 = permute(x1, partner)
    y2 = permute(x2, partner)
    y0k = permute(x0k, partner)
    own0s, own_sq0s = own0s_call(mine, salt, *params)
    q, salts, sq_query = query_call(queries, yq, salt, other_salt, *params)
    own1, own2, own0k, own_sq = own_rest_call(mine, salt, *params)

    def gram(slot, part, own, other, squares, *more):
        return gram_call(slot, part, own, other, q, salts, *params, squares, *more)

    everything = range(8)
    send0, sq0s = gram(0, range(4), own0s, y0s, own_sq0s)
    send1, keep1, sq1 = gram(1, everything, own1, y1, own_sq)
    send2, keep2 = gram(2, everything, own2, y2, own_sq, sq_query, sq0s, y0k, sq1)
    keep0, _ = gram(0, range(4, 8), own0k, y0k, own_sq)
    sends, keeps, gots = [send0, send1, send2], [keep0, keep1, keep2], [None] * 3
    none = [0, 0, 0]
    for step in range(6):
        half = 16 >> step
        for slot in range(3):
            turn = axis_bits(slot + step)
            pairs = moves(turn, none) if step < 3 else moves(none, turn)
            got = permute(sends[slot], pairs)
            kept = keeps[slot]
            if step < 5:
                sends[slot] = kept[half:] + got[half:]
                keeps[slot] = kept[:half] + got[:half]
            else:
                gots[slot] = got
    send, keep = last_sum_call(keeps, gots)
    return finish_call(keep, permute(send, partner))


def solution(mesh):
    placed = (P(AXES, None), P(AXES), P(), P(), P())
    return jax.shard_map(
        body, mesh=mesh, in_specs=placed, out_specs=P("rows", "tiles"), check_vma=False
    )
```

time: 81.5 us -> 98.5 us (1.21)
  waiting for transfers between devices: 26 us -> 47.5 us
  starting transfers between devices: 43.2 us -> 39.5 us
  local copies, waits for them, and re-layouts: 2.85 us -> 0.02 us
  Pallas kernels: 8.32 us -> 10 us
    ppermute x22 -> x25, waiting for transfers between devices: 26 us -> 47.5 us  [permute(): return lax.ppermute(x, AXES, pairs)]
    ppermute x22 -> x25, starting transfers between devices: 43.2 us -> 39.5 us  [permute(): return lax.ppermute(x, AXES, pairs)]
    unnamed x10 -> x8, local copies, waits for them, and re-layouts: 2.85 us -> 0.02 us
    pallas_call x3, Pallas kernels: 3.35 us -> 4.75 us  [the longest x1 2.39 us: cast_call(): call(cast_kernel, [((128, 256), f32), ((4, 128, 384), f32), ((8, 128, 384...]
  transfers between devices with their start and end apart: 22 -> 25, of which waited for: 14 -> 15; matrix products, arithmetic and copies ran while one was open for 1% -> 1% of each run, Pallas kernels for 8% -> 7%
where the time goes in v2:
time: 98.5 us; the launch traced here: 98.4 us
  waiting for transfers between devices  47.5 us (48%)
  starting transfers between devices  39.5 us (40%)
  Pallas kernels  10 us (10%)
  other arithmetic  1.15 us (1%)
    ppermute x25, waiting for transfers between devices, permute(): return lax.ppermute(x, AXES, pairs)  47.5 us
    ppermute x25, starting transfers between devices, permute(): return lax.ppermute(x, AXES, pairs)  39.5 us
    pallas_call x4, Pallas kernels, gram_call(): call(functools.partial(kernel, slot, part), out_shape, 'v' * (8 + len(mor...  4.19 us
    pallas_call x1, Pallas kernels, cast_call(): call(cast_kernel, [((128, 256), f32), ((4, 128, 384), f32), ((8, 128, 384...  2.39 us
  transfers between devices with their start and end apart: 25, of which 15 were waited for; matrix products, arithmetic and copies ran while one was open for 1% of the time, Pallas kernels for 7%

profile of v2, /device:TPU:1, one launch (start us, length us, event | category | flops | bytes accessed | tf_op | source)
XLA Modules:
  0.0 98.4 jit_solution(21135224583820119)
XLA Ops:
  0.0 2.4 %shard_map.55 = (f32[128,256]{1,0:T(8,128)S(1)}, f32[4,128,384]{2,1,0:T(8,128)S(1)}, f32[8,128,384]{2,1,0:T(8,128)S(1)}, f32[8,128,256]{2,1,0:T(8,128)S(1)}, f32...) custom-call(bf16[128,16384]{1,0:T(8,128)(2,1)} %feat.1), custom_call_target="tpu_custom_call" | custom-call | flops 1000000 | bytes 6291456 | tf_op jit(solution)/shard_map/pallas_call | solution.py:112
  2.4 1.4 %collective-permute-start.3 = (f32[4,128,384]{2,1,0:T(8,128)S(1)}, f32[4,128,384]{2,1,0:T(8,128)S(1)}, u32[]{:S(2)}, u32[]{:S(2)}) collective-permute-start(f32[4,128,384]{2,1,0:T(8,128)S(1)} %get-tuple-element.41), channel_id=1, source_target_pairs={{0,8},{1,9},{2,10},{3,11},{4,12},{5,13},{6,14},{7,15},{8,0},{9,1},... | collective-permute-start | bytes 2359304 | tf_op jit(solution)/shard_map/ppermute | solution.py:370
  3.9 0.1 collective-permute-start.9
  3.9 0.4 collective-permute-start.1
  4.4 0.1 collective-permute-start.2
  4.5 0.5 shard_map.59
  4.9 3.3 %collective-permute-done.2.other_salt = s32[1,128]{1,0:T(1,128)S(1)} collective-permute-done((s32[1,128]{1,0:T(1,128)S(1)}, s32[1,128]{1,0:T(1,128)S(1)}, u32[]{:S(2)}, u32[]{:S(2)}) %collective-permute-start.2) | collective-permute-done | bytes 544 | tf_op jit(solution)/shard_map/ppermute | solution.py:370
  8.2 0.3 shard_map.57
  8.5 0.7 shard_map.60
  9.3 2.7 %collective-permute-start.4 = (f32[32,96,128]{2,1,0:T(8,128)S(1)}, f32[32,96,128]{2,1,0:T(8,128)S(1)}, u32[]{:S(2)}, u32[]{:S(2)}) collective-permute-start(f32[32,96,128]{2,1,0:T(8,128)S(1)} %get-tuple-element.43), channel_id=1, source_target_pairs={{0,1},{1,0},{2,3},{3,2},{4,5},{5,4},{6,7},{7,6},{8,11},{9,10},{10,... | collective-permute-start | bytes 4718600 | tf_op jit(solution)/shard_map/ppermute | solution.py:370
  12.0 0.5 collective-permute-start.15
  12.5 1.9 %shard_map.56 = (bf16[8,128,384]{2,1,0:T(8,128)(2,1)S(1)}, bf16[8,128,256]{2,1,0:T(8,128)(2,1)S(1)}, bf16[4,128,384]{2,1,0:T(8,128)(2,1)S(1)}, f32[8,8,128]{2,1,0:T(8,128)S(1)}) custom-call(bf16[8,128,1024]{2,1,0:T(8,128)(2,1)S(1)} %get-tuple-element.31.mine, s32[1,128]{1,0:T(1,128)S(1)} %bitcast.28, s32[128,128]{1,0:T(8,128)S(1)} %bitcast.7, ...), custom_call_target="tpu_custom_call" | custom-call | flops 16000000 | bytes 4194304 | tf_op jit(solution)/shard_map/pallas_call | solution.py:182
  14.4 1.3 %shard_map.61 = (f32[32,96,128]{2,1,0:T(8,128)S(1)}, f32[32,96,128]{2,1,0:T(8,128)S(1)}, f32[8,8,128]{2,1,0:T(8,128)S(1)}) custom-call(bf16[8,128,384]{2,1,0:T(8,128)(2,1)S(1)} %get-tuple-element.44.own, f32[8,128,384]{2,1,0:T(8,128)S(1)} %collective-permute-done.9.other, bf16[2,256,256]{2,1,0:T(8,128)(2,1)S(1)} %get-tuple-element.36.q, ...), custom_call_target="tpu_custom_call" | custom-call | flops 384000000 | bytes 5242880 | tf_op jit(solution)/shard_map/pallas_call | solution.py:315
  15.7 2.8 %collective-permute-start.10 = (f32[32,96,128]{2,1,0:T(8,128)S(1)}, f32[32,96,128]{2,1,0:T(8,128)S(1)}, u32[]{:S(2)}, u32[]{:S(2)}) collective-permute-start(f32[32,96,128]{2,1,0:T(8,128)S(1)} %get-tuple-element.47), channel_id=1, source_target_pairs={{0,4},{1,5},{2,6},{3,7},{4,0},{5,1},{6,2},{7,3},{8,76},{9,77},{10,... | collective-permute-start | bytes 4718600 | tf_op jit(solution)/shard_map/ppermute | solution.py:370
  18.5 1.2 %shard_map.58 = (f32[32,96,128]{2,1,0:T(8,128)S(1)}, f32[4,8,128]{2,1,0:T(8,128)}) custom-call(bf16[4,128,384]{2,1,0:T(8,128)(2,1)S(1)} %get-tuple-element.32.own, f32[4,128,384]{2,1,0:T(8,128)S(1)} %collective-permute-done.other.other0k, bf16[2,256,256]{2,1,0:T(8,128)(2,1)S(1)} %get-tuple-element.36.q, s32[128,128]{1,0:T(8,128)S(1)} %get-tuple-element.37.salt, ...), custom_call_target="tpu_custom_call" | custom-call | flops 192000000 | bytes 5242880 | tf_op jit(solution)/shard_map/pallas_call | solution.py:315
  19.7 10.1 %collective-permute-done.4 = f32[32,96,128]{2,1,0:T(8,128)S(1)} collective-permute-done((f32[32,96,128]{2,1,0:T(8,128)S(1)}, f32[32,96,128]{2,1,0:T(8,128)S(1)}, u32[]{:S(2)}, u32[]{:S(2)}) %collective-permute-start.4) | collective-permute-done | bytes 1572896 | tf_op jit(solution)/shard_map/ppermute | solution.py:370
  29.8 0.3 slice_add_fusion.3
  30.1 3.0 %collective-permute-start.5 = (f32[16,96,128]{2,1,0:T(8,128)S(1)}, f32[16,96,128]{2,1,0:T(8,128)S(1)}, u32[]{:S(2)}, u32[]{:S(2)}) collective-permute-start(f32[16,96,128]{2,1,0:T(8,128)S(1)} %get-tuple-element.60), channel_id=1, source_target_pairs={{0,4},{1,5},{2,6},{3,7},{4,0},{5,1},{6,2},{7,3},{8,76},{9,77},{10,... | collective-permute-start | bytes 2359304 | tf_op jit(solution)/shard_map/ppermute | solution.py:370
  33.0 1.0 shard_map.62
  34.0 3.8 %collective-permute-start.16 = (f32[32,80,128]{2,1,0:T(8,128)S(1)}, f32[32,80,128]{2,1,0:T(8,128)S(1)}, u32[]{:S(2)}, u32[]{:S(2)}) collective-permute-start(f32[32,80,128]{2,1,0:T(8,128)S(1)} %get-tuple-element.54), channel_id=1, source_target_pairs={{0,16},{1,17},{2,18},{3,19},{4,20},{5,21},{6,22},{7,23},{8,56},{9,... | collective-permute-start | bytes 3932168 | tf_op jit(solution)/shard_map/ppermute | solution.py:370
  37.8 6.9 %collective-permute-done.5 = f32[16,96,128]{2,1,0:T(8,128)S(1)} collective-permute-done((f32[16,96,128]{2,1,0:T(8,128)S(1)}, f32[16,96,128]{2,1,0:T(8,128)S(1)}, u32[]{:S(2)}, u32[]{:S(2)}) %collective-permute-start.5) | collective-permute-done | bytes 786464 | tf_op jit(solution)/shard_map/ppermute | solution.py:370
  44.7 0.1 slice_add_fusion.9
  44.8 3.8 %collective-permute-start.6 = (f32[8,96,128]{2,1,0:T(8,128)S(1)}, f32[8,96,128]{2,1,0:T(8,128)S(1)}, u32[]{:S(2)}, u32[]{:S(2)}) collective-permute-start(f32[8,96,128]{2,1,0:T(8,128)S(1)} %get-tuple-element.66), channel_id=1, source_target_pairs={{0,16},{1,17},{2,18},{3,19},{4,20},{5,21},{6,22},{7,23},{8,56},{9,... | collective-permute-start | bytes 1179656 | tf_op jit(solution)/shard_map/ppermute | solution.py:370
  48.7 0.2 slice_add_fusion.1
  48.9 0.1 collective-permute-start.11
  49.0 8.1 %collective-permute-done.6 = f32[8,96,128]{2,1,0:T(8,128)S(1)} collective-permute-done((f32[8,96,128]{2,1,0:T(8,128)S(1)}, f32[8,96,128]{2,1,0:T(8,128)S(1)}, u32[]{:S(2)}, u32[]{:S(2)}) %collective-permute-start.6) | collective-permute-done | bytes 393248 | tf_op jit(solution)/shard_map/ppermute | solution.py:370
  57.1 0.4 collective-permute-start.7
  57.5 0.2 slice_add_fusion.5
  57.7 2.3 %collective-permute-start.17 = (f32[16,80,128]{2,1,0:T(8,128)S(1)}, f32[16,80,128]{2,1,0:T(8,128)S(1)}, u32[]{:S(2)}, u32[]{:S(2)}) collective-permute-start(f32[16,80,128]{2,1,0:T(8,128)S(1)} %get-tuple-element.62), channel_id=1, source_target_pairs={{0,1},{1,0},{2,3},{3,2},{4,5},{5,4},{6,7},{7,6},{8,11},{9,10},{10,... | collective-permute-start | bytes 1966088 | tf_op jit(solution)/shard_map/ppermute | solution.py:370
  59.9 2.7 %collective-permute-done.7 = f32[4,96,128]{2,1,0:T(8,128)S(1)} collective-permute-done((f32[4,96,128]{2,1,0:T(8,128)S(1)}, f32[4,96,128]{2,1,0:T(8,128)S(1)}, u32[]{:S(2)}, u32[]{:S(2)}) %collective-permute-start.7) | collective-permute-done | bytes 196640 | tf_op jit(solution)/shard_map/ppermute | solution.py:370
  62.7 2.7 %collective-permute-done.11 = f32[16,96,128]{2,1,0:T(8,128)S(1)} collective-permute-done((f32[16,96,128]{2,1,0:T(8,128)S(1)}, f32[16,96,128]{2,1,0:T(8,128)S(1)}, u32[]{:S(2)}, u32[]{:S(2)}) %collective-permute-start.11) | collective-permute-done | bytes 786464 | tf_op jit(solution)/shard_map/ppermute | solution.py:370
  65.5 0.1 slice_add_fusion.7
  65.6 2.5 %collective-permute-start.12 = (f32[8,96,128]{2,1,0:T(8,128)S(1)}, f32[8,96,128]{2,1,0:T(8,128)S(1)}, u32[]{:S(2)}, u32[]{:S(2)}) collective-permute-start(f32[8,96,128]{2,1,0:T(8,128)S(1)} %get-tuple-element.64), channel_id=1, source_target_pairs={{0,1},{1,0},{2,3},{3,2},{4,5},{5,4},{6,7},{7,6},{8,11},{9,10},{10,... | collective-permute-start | bytes 1179656 | tf_op jit(solution)/shard_map/ppermute | solution.py:370
  68.1 0.3 collective-permute-done.17
  68.5 2.2 %collective-permute-start.18 = (f32[8,80,128]{2,1,0:T(8,128)S(1)}, f32[8,80,128]{2,1,0:T(8,128)S(1)}, u32[]{:S(2)}, u32[]{:S(2)}) collective-permute-start(f32[8,80,128]{2,1,0:T(8,128)S(1)} %get-tuple-element.68), channel_id=1, source_target_pairs={{0,4},{1,5},{2,6},{3,7},{4,0},{5,1},{6,2},{7,3},{8,76},{9,77},{10,... | collective-permute-start | bytes 983048 | tf_op jit(solution)/shard_map/ppermute | solution.py:370
  70.9 2.6 %collective-permute-done.12 = f32[8,96,128]{2,1,0:T(8,128)S(1)} collective-permute-done((f32[8,96,128]{2,1,0:T(8,128)S(1)}, f32[8,96,128]{2,1,0:T(8,128)S(1)}, u32[]{:S(2)}, u32[]{:S(2)}) %collective-permute-start.12) | collective-permute-done | bytes 393248 | tf_op jit(solution)/shard_map/ppermute | solution.py:370
  73.6 2.1 %collective-permute-done.18 = f32[8,80,128]{2,1,0:T(8,128)S(1)} collective-permute-done((f32[8,80,128]{2,1,0:T(8,128)S(1)}, f32[8,80,128]{2,1,0:T(8,128)S(1)}, u32[]{:S(2)}, u32[]{:S(2)}) %collective-permute-start.18) | collective-permute-done | bytes 327712 | tf_op jit(solution)/shard_map/ppermute | solution.py:370
  75.8 2.0 %collective-permute-start.19 = (f32[4,80,128]{2,1,0:T(8,128)S(1)}, f32[4,80,128]{2,1,0:T(8,128)S(1)}, u32[]{:S(2)}, u32[]{:S(2)}) collective-permute-start(f32[4,80,128]{2,1,0:T(8,128)S(1)} %get-tuple-element.74), channel_id=1, source_target_pairs={{0,48},{1,49},{2,50},{3,51},{4,52},{5,53},{6,54},{7,55},{8,24},{9,... | collective-permute-start | bytes 491528 | tf_op jit(solution)/shard_map/ppermute | solution.py:370
  77.7 0.4 collective-permute-done.13
  78.2 1.0 %collective-permute-start.14 = (f32[2,96,128]{2,1,0:T(8,128)S(1)}, f32[2,96,128]{2,1,0:T(8,128)S(1)}, u32[]{:S(2)}, u32[]{:S(2)}) collective-permute-start(f32[2,96,128]{2,1,0:T(8,128)S(1)} %get-tuple-element.76), channel_id=1, source_target_pairs={{0,48},{1,49},{2,50},{3,51},{4,52},{5,53},{6,54},{7,55},{8,24},{9,... | collective-permute-start | bytes 294920 | tf_op jit(solution)/shard_map/ppermute | solution.py:370
  79.2 1.6 %collective-permute-done.19 = f32[4,80,128]{2,1,0:T(8,128)S(1)} collective-permute-done((f32[4,80,128]{2,1,0:T(8,128)S(1)}, f32[4,80,128]{2,1,0:T(8,128)S(1)}, u32[]{:S(2)}, u32[]{:S(2)}) %collective-permute-start.19) | collective-permute-done | bytes 163872 | tf_op jit(solution)/shard_map/ppermute | solution.py:370
  80.9 1.1 %collective-permute-done.14 = f32[2,96,128]{2,1,0:T(8,128)S(1)} collective-permute-done((f32[2,96,128]{2,1,0:T(8,128)S(1)}, f32[2,96,128]{2,1,0:T(8,128)S(1)}, u32[]{:S(2)}, u32[]{:S(2)}) %collective-permute-start.14) | collective-permute-done | bytes 98336 | tf_op jit(solution)/shard_map/ppermute | solution.py:370
  82.0 0.6 collective-permute-start.22
  82.6 1.5 %collective-permute-done.20 = f32[2,80,128]{2,1,0:T(8,128)S(1)} collective-permute-done((f32[2,80,128]{2,1,0:T(8,128)S(1)}, f32[2,80,128]{2,1,0:T(8,128)S(1)}, u32[]{:S(2)}, u32[]{:S(2)}) %collective-permute-start.20) | collective-permute-done | bytes 81952 | tf_op jit(solution)/shard_map/ppermute | solution.py:370
  84.3 3.1 %collective-permute-done.23.got2 = f32[1,80,128]{2,1,0:T(8,128)S(1)} collective-permute-done((f32[1,80,128]{2,1,0:T(8,128)S(1)}, f32[1,80,128]{2,1,0:T(8,128)S(1)}, u32[]{:S(2)}, u32[]{:S(2)}) %collective-permute-start.23) | collective-permute-done | bytes 40992 | tf_op jit(solution)/shard_map/ppermute | solution.py:370
  87.4 9.3 %collective-permute-start.24 = (f32[136,128]{1,0:T(8,128)S(1)}, f32[136,128]{1,0:T(8,128)S(1)}, u32[]{:S(2)}, u32[]{:S(2)}) collective-permute-start(f32[136,128]{1,0:T(8,128)S(1)} %get-tuple-element.56), channel_id=1, source_target_pairs={{0,8},{1,9},{2,10},{3,11},{4,12},{5,13},{6,14},{7,15},{8,0},{9,1},... | collective-permute-start | bytes 208904 | tf_op jit(solution)/shard_map/ppermute | solution.py:370
  96.7 0.9 collective-permute-done.24.other
  97.6 0.8 shard_map.64
  (35 shorter events, 0.8 us)
Async XLA Ops:
  0.0 4.4 %copy-start.3 = (s32[128]{0:T(128)S(1)}, s32[128]{0:T(128)}, u32[]{:S(2)}) copy-start(s32[128]{0:T(128)} %param.6) | copy-start | bytes 1540
  0.0 4.5 %copy-start = (s32[16384]{0:T(1024)S(1)}, s32[16384]{0:T(1024)}, u32[]{:S(2)}) copy-start(s32[16384]{0:T(1024)} %param.7) | copy-start | bytes 196612
  0.0 4.5 %copy-start.1 = (s32[16384]{0:T(1024)S(1)}, s32[16384]{0:T(1024)}, u32[]{:S(2)}) copy-start(s32[16384]{0:T(1024)} %param.8) | copy-start | bytes 196612
  0.0 4.5 %copy-start.2 = (s32[16384]{0:T(1024)S(1)}, s32[16384]{0:T(1024)}, u32[]{:S(2)}) copy-start(s32[16384]{0:T(1024)} %param.9) | copy-start | bytes 196612
  2.4 6.1 %collective-permute-start.3 = (f32[4,128,384]{2,1,0:T(8,128)S(1)}, f32[4,128,384]{2,1,0:T(8,128)S(1)}, u32[]{:S(2)}, u32[]{:S(2)}) collective-permute-start(f32[4,128,384]{2,1,0:T(8,128)S(1)} %get-tuple-element.41), channel_id=1, source_target_pairs={{0,8},{1,9},{2,10},{3,11},{4,12},{5,13},{6,14},{7,15},{8,0},{9,1},... | collective-permute-start | bytes 2359304 | tf_op jit(solution)/shard_map/ppermute | solution.py:370
  3.9 10.5 %collective-permute-start.9 = (f32[8,128,384]{2,1,0:T(8,128)S(1)}, f32[8,128,384]{2,1,0:T(8,128)S(1)}, u32[]{:S(2)}, u32[]{:S(2)}) collective-permute-start(f32[8,128,384]{2,1,0:T(8,128)S(1)} %get-tuple-element.45), channel_id=1, source_target_pairs={{0,8},{1,9},{2,10},{3,11},{4,12},{5,13},{6,14},{7,15},{8,0},{9,1},... | collective-permute-start | bytes 4718600 | tf_op jit(solution)/shard_map/ppermute | solution.py:370
  3.9 4.3 %collective-permute-start.1 = (f32[128,256]{1,0:T(8,128)S(1)}, f32[128,256]{1,0:T(8,128)S(1)}, u32[]{:S(2)}, u32[]{:S(2)}) collective-permute-start(f32[128,256]{1,0:T(8,128)S(1)} %get-tuple-element.35), channel_id=1, source_target_pairs={{0,8},{1,9},{2,10},{3,11},{4,12},{5,13},{6,14},{7,15},{8,0},{9,1},... | collective-permute-start | bytes 393224 | tf_op jit(solution)/shard_map/ppermute | solution.py:370
  4.4 3.8 %collective-permute-start.2 = (s32[1,128]{1,0:T(1,128)S(1)}, s32[1,128]{1,0:T(1,128)S(1)}, u32[]{:S(2)}, u32[]{:S(2)}) collective-permute-start(s32[1,128]{1,0:T(1,128)S(1)} %bitcast.25), channel_id=1, source_target_pairs={{0,8},{1,9},{2,10},{3,11},{4,12},{5,13},{6,14},{7,15},{8,0},{9,1},... | collective-permute-start | bytes 1544 | tf_op jit(solution)/shard_map/ppermute | solution.py:370
  9.3 20.6 %collective-permute-start.4 = (f32[32,96,128]{2,1,0:T(8,128)S(1)}, f32[32,96,128]{2,1,0:T(8,128)S(1)}, u32[]{:S(2)}, u32[]{:S(2)}) collective-permute-start(f32[32,96,128]{2,1,0:T(8,128)S(1)} %get-tuple-element.43), channel_id=1, source_target_pairs={{0,1},{1,0},{2,3},{3,2},{4,5},{5,4},{6,7},{7,6},{8,11},{9,10},{10,... | collective-permute-start | bytes 4718600 | tf_op jit(solution)/shard_map/ppermute | solution.py:370
  12.0 6.5 %collective-permute-start = (f32[4,128,384]{2,1,0:T(8,128)S(1)}, f32[4,128,384]{2,1,0:T(8,128)S(1)}, u32[]{:S(2)}, u32[]{:S(2)}) collective-permute-start(f32[4,128,384]{2,1,0:T(8,128)S(1)} %get-tuple-element.33), channel_id=1, source_target_pairs={{0,8},{1,9},{2,10},{3,11},{4,12},{5,13},{6,14},{7,15},{8,0},{9,1},... | collective-permute-start | bytes 2359304 | tf_op jit(solution)/shard_map/ppermute | solution.py:370
  12.0 21.1 %collective-permute-start.15 = (f32[8,128,256]{2,1,0:T(8,128)S(1)}, f32[8,128,256]{2,1,0:T(8,128)S(1)}, u32[]{:S(2)}, u32[]{:S(2)}) collective-permute-start(f32[8,128,256]{2,1,0:T(8,128)S(1)} %get-tuple-element.49), channel_id=1, source_target_pairs={{0,8},{1,9},{2,10},{3,11},{4,12},{5,13},{6,14},{7,15},{8,0},{9,1},... | collective-permute-start | bytes 3145736 | tf_op jit(solution)/shard_map/ppermute | solution.py:370
  15.7 33.0 %collective-permute-start.10 = (f32[32,96,128]{2,1,0:T(8,128)S(1)}, f32[32,96,128]{2,1,0:T(8,128)S(1)}, u32[]{:S(2)}, u32[]{:S(2)}) collective-permute-start(f32[32,96,128]{2,1,0:T(8,128)S(1)} %get-tuple-element.47), channel_id=1, source_target_pairs={{0,4},{1,5},{2,6},{3,7},{4,0},{5,1},{6,2},{7,3},{8,76},{9,77},{10,... | collective-permute-start | bytes 4718600 | tf_op jit(solution)/shard_map/ppermute | solution.py:370
  30.1 14.7 %collective-permute-start.5 = (f32[16,96,128]{2,1,0:T(8,128)S(1)}, f32[16,96,128]{2,1,0:T(8,128)S(1)}, u32[]{:S(2)}, u32[]{:S(2)}) collective-permute-start(f32[16,96,128]{2,1,0:T(8,128)S(1)} %get-tuple-element.60), channel_id=1, source_target_pairs={{0,4},{1,5},{2,6},{3,7},{4,0},{5,1},{6,2},{7,3},{8,76},{9,77},{10,... | collective-permute-start | bytes 2359304 | tf_op jit(solution)/shard_map/ppermute | solution.py:370
  34.0 23.5 %collective-permute-start.16 = (f32[32,80,128]{2,1,0:T(8,128)S(1)}, f32[32,80,128]{2,1,0:T(8,128)S(1)}, u32[]{:S(2)}, u32[]{:S(2)}) collective-permute-start(f32[32,80,128]{2,1,0:T(8,128)S(1)} %get-tuple-element.54), channel_id=1, source_target_pairs={{0,16},{1,17},{2,18},{3,19},{4,20},{5,21},{6,22},{7,23},{8,56},{9,... | collective-permute-start | bytes 3932168 | tf_op jit(solution)/shard_map/ppermute | solution.py:370
  44.8 12.2 %collective-permute-start.6 = (f32[8,96,128]{2,1,0:T(8,128)S(1)}, f32[8,96,128]{2,1,0:T(8,128)S(1)}, u32[]{:S(2)}, u32[]{:S(2)}) collective-permute-start(f32[8,96,128]{2,1,0:T(8,128)S(1)} %get-tuple-element.66), channel_id=1, source_target_pairs={{0,16},{1,17},{2,18},{3,19},{4,20},{5,21},{6,22},{7,23},{8,56},{9,... | collective-permute-start | bytes 1179656 | tf_op jit(solution)/shard_map/ppermute | solution.py:370
  48.9 16.6 %collective-permute-start.11 = (f32[16,96,128]{2,1,0:T(8,128)S(1)}, f32[16,96,128]{2,1,0:T(8,128)S(1)}, u32[]{:S(2)}, u32[]{:S(2)}) collective-permute-start(f32[16,96,128]{2,1,0:T(8,128)S(1)} %get-tuple-element.58), channel_id=1, source_target_pairs={{0,16},{1,17},{2,18},{3,19},{4,20},{5,21},{6,22},{7,23},{8,56},{9,... | collective-permute-start | bytes 2359304 | tf_op jit(solution)/shard_map/ppermute | solution.py:370
  57.1 5.5 %collective-permute-start.7 = (f32[4,96,128]{2,1,0:T(8,128)S(1)}, f32[4,96,128]{2,1,0:T(8,128)S(1)}, u32[]{:S(2)}, u32[]{:S(2)}) collective-permute-start(f32[4,96,128]{2,1,0:T(8,128)S(1)} %get-tuple-element.72), channel_id=1, source_target_pairs={{0,3},{1,2},{2,1},{3,0},{4,7},{5,6},{6,5},{7,4},{8,9},{9,8},{10,11... | collective-permute-start | bytes 589832 | tf_op jit(solution)/shard_map/ppermute | solution.py:370
  57.7 10.8 %collective-permute-start.17 = (f32[16,80,128]{2,1,0:T(8,128)S(1)}, f32[16,80,128]{2,1,0:T(8,128)S(1)}, u32[]{:S(2)}, u32[]{:S(2)}) collective-permute-start(f32[16,80,128]{2,1,0:T(8,128)S(1)} %get-tuple-element.62), channel_id=1, source_target_pairs={{0,1},{1,0},{2,3},{3,2},{4,5},{5,4},{6,7},{7,6},{8,11},{9,10},{10,... | collective-permute-start | bytes 1966088 | tf_op jit(solution)/shard_map/ppermute | solution.py:370
  62.6 8.1 %collective-permute-start.8 = (f32[2,96,128]{2,1,0:T(8,128)S(1)}, f32[2,96,128]{2,1,0:T(8,128)S(1)}, u32[]{:S(2)}, u32[]{:S(2)}) collective-permute-start(f32[2,96,128]{2,1,0:T(8,128)S(1)} %get-tuple-element.78), channel_id=1, source_target_pairs={{0,68},{1,69},{2,70},{3,71},{4,64},{5,65},{6,66},{7,67},{8,12},{9,... | collective-permute-start | bytes 294920 | tf_op jit(solution)/shard_map/ppermute | solution.py:370
  65.6 7.9 %collective-permute-start.12 = (f32[8,96,128]{2,1,0:T(8,128)S(1)}, f32[8,96,128]{2,1,0:T(8,128)S(1)}, u32[]{:S(2)}, u32[]{:S(2)}) collective-permute-start(f32[8,96,128]{2,1,0:T(8,128)S(1)} %get-tuple-element.64), channel_id=1, source_target_pairs={{0,1},{1,0},{2,3},{3,2},{4,5},{5,4},{6,7},{7,6},{8,11},{9,10},{10,... | collective-permute-start | bytes 1179656 | tf_op jit(solution)/shard_map/ppermute | solution.py:370
  68.5 7.2 %collective-permute-start.18 = (f32[8,80,128]{2,1,0:T(8,128)S(1)}, f32[8,80,128]{2,1,0:T(8,128)S(1)}, u32[]{:S(2)}, u32[]{:S(2)}) collective-permute-start(f32[8,80,128]{2,1,0:T(8,128)S(1)} %get-tuple-element.68), channel_id=1, source_target_pairs={{0,4},{1,5},{2,6},{3,7},{4,0},{5,1},{6,2},{7,3},{8,76},{9,77},{10,... | collective-permute-start | bytes 983048 | tf_op jit(solution)/shard_map/ppermute | solution.py:370
  70.8 13.5 %collective-permute-start.21 = (f32[1,96,128]{2,1,0:T(8,128)S(1)}, f32[1,96,128]{2,1,0:T(8,128)S(1)}, u32[]{:S(2)}, u32[]{:S(2)}) collective-permute-start(f32[1,96,128]{2,1,0:T(8,128)S(1)} %get-tuple-element.83), channel_id=1, source_target_pairs={{0,48},{1,49},{2,50},{3,51},{4,52},{5,53},{6,54},{7,55},{8,24},{9,... | collective-permute-start | bytes 147464 | tf_op jit(solution)/shard_map/ppermute | solution.py:370
  73.5 4.6 %collective-permute-start.13 = (f32[4,96,128]{2,1,0:T(8,128)S(1)}, f32[4,96,128]{2,1,0:T(8,128)S(1)}, u32[]{:S(2)}, u32[]{:S(2)}) collective-permute-start(f32[4,96,128]{2,1,0:T(8,128)S(1)} %get-tuple-element.70), channel_id=1, source_target_pairs={{0,68},{1,69},{2,70},{3,71},{4,64},{5,65},{6,66},{7,67},{8,12},{9,... | collective-permute-start | bytes 589832 | tf_op jit(solution)/shard_map/ppermute | solution.py:370
  75.8 5.0 %collective-permute-start.19 = (f32[4,80,128]{2,1,0:T(8,128)S(1)}, f32[4,80,128]{2,1,0:T(8,128)S(1)}, u32[]{:S(2)}, u32[]{:S(2)}) collective-permute-start(f32[4,80,128]{2,1,0:T(8,128)S(1)} %get-tuple-element.74), channel_id=1, source_target_pairs={{0,48},{1,49},{2,50},{3,51},{4,52},{5,53},{6,54},{7,55},{8,24},{9,... | collective-permute-start | bytes 491528 | tf_op jit(solution)/shard_map/ppermute | solution.py:370
  78.2 3.8 %collective-permute-start.14 = (f32[2,96,128]{2,1,0:T(8,128)S(1)}, f32[2,96,128]{2,1,0:T(8,128)S(1)}, u32[]{:S(2)}, u32[]{:S(2)}) collective-permute-start(f32[2,96,128]{2,1,0:T(8,128)S(1)} %get-tuple-element.76), channel_id=1, source_target_pairs={{0,48},{1,49},{2,50},{3,51},{4,52},{5,53},{6,54},{7,55},{8,24},{9,... | collective-permute-start | bytes 294920 | tf_op jit(solution)/shard_map/ppermute | solution.py:370
  80.8 3.4 %collective-permute-start.20 = (f32[2,80,128]{2,1,0:T(8,128)S(1)}, f32[2,80,128]{2,1,0:T(8,128)S(1)}, u32[]{:S(2)}, u32[]{:S(2)}) collective-permute-start(f32[2,80,128]{2,1,0:T(8,128)S(1)} %get-tuple-element.80), channel_id=1, source_target_pairs={{0,3},{1,2},{2,1},{3,0},{4,7},{5,6},{6,5},{7,4},{8,9},{9,8},{10,11... | collective-permute-start | bytes 245768 | tf_op jit(solution)/shard_map/ppermute | solution.py:370
  82.0 5.4 %collective-permute-start.22 = (f32[1,96,128]{2,1,0:T(8,128)S(1)}, f32[1,96,128]{2,1,0:T(8,128)S(1)}, u32[]{:S(2)}, u32[]{:S(2)}) collective-permute-start(f32[1,96,128]{2,1,0:T(8,128)S(1)} %get-tuple-element.81), channel_id=1, source_target_pairs={{0,3},{1,2},{2,1},{3,0},{4,7},{5,6},{6,5},{7,4},{8,9},{9,8},{10,11... | collective-permute-start | bytes 147464 | tf_op jit(solution)/shard_map/ppermute | solution.py:370
  84.2 3.2 %collective-permute-start.23 = (f32[1,80,128]{2,1,0:T(8,128)S(1)}, f32[1,80,128]{2,1,0:T(8,128)S(1)}, u32[]{:S(2)}, u32[]{:S(2)}) collective-permute-start(f32[1,80,128]{2,1,0:T(8,128)S(1)} %get-tuple-element.85), channel_id=1, source_target_pairs={{0,68},{1,69},{2,70},{3,71},{4,64},{5,65},{6,66},{7,67},{8,12},{9,... | collective-permute-start | bytes 122888 | tf_op jit(solution)/shard_map/ppermute | solution.py:370
  87.4 10.2 %collective-permute-start.24 = (f32[136,128]{1,0:T(8,128)S(1)}, f32[136,128]{1,0:T(8,128)S(1)}, u32[]{:S(2)}, u32[]{:S(2)}) collective-permute-start(f32[136,128]{1,0:T(8,128)S(1)} %get-tuple-element.56), channel_id=1, source_target_pairs={{0,8},{1,9},{2,10},{3,11},{4,12},{5,13},{6,14},{7,15},{8,0},{9,1},... | collective-permute-start | bytes 208904 | tf_op jit(solution)/shard_map/ppermute | solution.py:370

commit v3 on v2

v3 whole, which is shorter than its diff:
```python
import functools

import jax
import jax.numpy as jnp
from jax import lax
from jax.experimental import pallas as pl
from jax.experimental.pallas import tpu as pltpu
from jax.sharding import PartitionSpec as P

AXES = ("rows", "tiles")
PRIME = 65521
SLOT_TILES = ((0, 1, 2), (3, 4, 5), (6, 7))
SLOT_ROWS = (96, 96, 80)


def place(index):
    rows, tiles = divmod(index, 8)
    return [tiles & 3, (rows >> 3) * 2 + (tiles >> 2), (rows >> 1) & 3], rows & 1


def index_of(chip, core):
    x, y, z = chip
    return (((y >> 1) << 3) | (z << 1) | core) * 8 + ((y & 1) << 2 | x)


def gray(v):
    return v ^ (v >> 1)


def flip(index, first, last):
    chip, core = place(index)
    for axis in range(3):
        mask = first[axis] << (1 - core) | last[axis] << core
        chip[axis] = gray(gray(chip[axis]) ^ mask)
    return index_of(chip, core)


def moves(first, last):
    return [(i, flip(i, first, last)) for i in range(128)]


def axis_bits(axis):
    return [int(a == axis % 3) for a in range(3)]


def my_place():
    rows = lax.axis_index("rows")
    tile = lax.axis_index("tiles")
    return rows & 1, rows >> 1, tile


def tile_at(core, tile, c, xa, xb):
    high = jnp.where(core == 1, xb, xa)
    return tile ^ (c * 4 + high * 2 + (xa ^ xb))


def weight_of(threshold):
    return lax.rsqrt(threshold.astype(jnp.float32) / 65521.0)


def fold(v):
    return v - (v >> 16) * PRIME


def sample(values, salt, multiplier, offset, threshold, weight):
    residue = fold(fold(salt * multiplier + offset))
    keep = (residue < threshold) | (residue >= PRIME)
    return jnp.where(keep, values * weight, 0.0).astype(jnp.bfloat16)


def call(kernel, out_shape, in_spaces, scratch=(), limit=16, flops=1_000_000, nbytes=1 << 20):
    spaces = {"v": pltpu.VMEM, "h": pltpu.HBM}
    return pl.pallas_call(
        kernel,
        out_shape=[jax.ShapeDtypeStruct(s, d) for s, d in out_shape],
        in_specs=[pl.BlockSpec(memory_space=spaces[s]) for s in in_spaces],
        out_specs=[pl.BlockSpec(memory_space=pltpu.VMEM)] * len(out_shape),
        scratch_shapes=list(scratch),
        compiler_params=pltpu.CompilerParams(vmem_limit_bytes=limit << 20),
        cost_estimate=pl.CostEstimate(flops=flops, bytes_accessed=nbytes, transcendentals=0),
    )


ORDER = [(xa, c, xb) for xa in (1, 0) for c in (0, 1) for xb in (0, 1)]


def cast_kernel(feat, outq, out0s, out1, out2, out0k, mine, queries, block, sems):
    core, _, tile = my_place()
    copies = [pltpu.make_async_copy(feat.at[:, 0:256], queries, sems.at[16])]
    for to, half, first in ((block, 1 - core, 0), (mine, core, 8)):
        for i, (xa, c, xb) in enumerate(ORDER):
            start = pl.multiple_of(tile_at(half, tile, c, xa, xb) * 2048 + half * 1024, 1024)
            copies.append(
                pltpu.make_async_copy(feat.at[:, pl.ds(start, 1024)], to.at[i], sems.at[first + i])
            )
    for copy in copies:
        copy.start()
    copies[0].wait()
    outq[...] = queries[...].astype(jnp.float32)
    for i in range(8):
        copies[1 + i].wait()
        out0 = out0s if i < 4 else out0k
        out0[i % 4] = block[i, :, 0:384].astype(jnp.float32)
        out1[i] = block[i, :, 384:768].astype(jnp.float32)
        out2[i] = block[i, :, 768:1024].astype(jnp.float32)
    for i in range(8):
        copies[9 + i].wait()


def cast_call(features):
    f32 = jnp.float32
    return call(
        cast_kernel,
        [
            ((128, 256), f32),
            ((4, 128, 384), f32),
            ((8, 128, 384), f32),
            ((8, 128, 256), f32),
            ((4, 128, 384), f32),
            ((8, 128, 1024), jnp.bfloat16),
            ((128, 256), jnp.bfloat16),
        ],
        "h",
        scratch=[
            pltpu.VMEM((8, 128, 1024), jnp.bfloat16),
            pltpu.SemaphoreType.DMA((17,)),
        ],
        limit=45,
        nbytes=6 << 20,
    )(features)


def column_of(row):
    return jnp.transpose(jnp.broadcast_to(row, (128, 128)))


def column_base(core, tile, i):
    xa, c, xb = ORDER[i]
    return tile_at(core, tile, c, xa, xb) * 16 + core * 8


def sum_squares(x):
    return jnp.sum(x * x, axis=0, keepdims=True)


def own_kernel(mine, salt, mult, offs, thr, out0s, out1, squares):
    core, _, tile = my_place()
    salts = column_of(salt[...])
    for i in range(8):
        outs = [(0, out0s), (1, out1)] if i < 4 else [(1, out1)]
        base = column_base(core, tile, i)
        for slot, out in outs:
            for k, l in enumerate(SLOT_TILES[slot]):
                m, o, t = (ref[pl.ds(base + l, 1), :] for ref in (mult, offs, thr))
                x = mine[i, :, l * 128 : (l + 1) * 128].astype(jnp.float32)
                squares[i, l : l + 1, :] = sum_squares(x)
                out[i, :, k * 128 : (k + 1) * 128] = sample(x, salts, m, o, t, weight_of(t))


def own_call(mine, salt, mult, offs, thr):
    return call(
        own_kernel,
        [
            ((4, 128, 384), jnp.bfloat16),
            ((8, 128, 384), jnp.bfloat16),
            ((8, 8, 128), jnp.float32),
        ],
        "vvvvv",
        limit=8,
        flops=12_000_000,
        nbytes=3 << 20,
    )(mine, salt, mult, offs, thr)


def query_kernel(
    queries, other, salt, other_salt, mult, offs, thr, q_out, salt_out, sq_out, q_all
):
    core, pair, _ = my_place()
    salts = (column_of(salt[...]), column_of(other_salt[...]))
    salt_out[0:128, :] = salts[0]
    salt_out[128:256, :] = salts[1]
    sq_out[...] = jnp.zeros_like(sq_out)
    for l in range(2):
        lanes = slice(l * 128, (l + 1) * 128)
        m, o, t = (ref[l : l + 1, :] for ref in (mult, offs, thr))
        w = weight_of(t)
        total = None
        for u in range(2):
            source = queries if u == 0 else other
            x = source[:, lanes].astype(jnp.float32)
            part = sum_squares(x)
            total = part if total is None else total + part
            value = sample(x, salts[u], m, o, t, w).astype(jnp.float32)
            q_all[lanes, u * 128 : (u + 1) * 128] = jnp.transpose(value).astype(jnp.bfloat16)
        sq_out[l : l + 1, :] = total
    for c in range(2):
        for group in range(8):
            ya, za, zb = group >> 2, group >> 1 & 1, group & 1
            z_high = jnp.where(core == 1, zb, za)
            y_high = jnp.where(core == 1, c ^ ya, ya)
            at = pair ^ (y_high * 4 + z_high * 2 + (za ^ zb))
            start = pl.multiple_of(at * 32, 32)
            q_out[c, group * 32 : (group + 1) * 32, :] = q_all[pl.ds(start, 32), :]


def query_call(queries, other, salt, other_salt, mult, offs, thr):
    return call(
        query_kernel,
        [
            ((2, 256, 256), jnp.bfloat16),
            ((256, 128), jnp.int32),
            ((8, 128), jnp.float32),
        ],
        "vvvvvvv",
        scratch=[pltpu.VMEM((256, 256), jnp.bfloat16)],
        limit=8,
        flops=4_000_000,
    )(queries, other, salt, other_salt, mult, offs, thr)


def gram_kernel(slot, own, other, q, salt, mult, offs, thr, own_sq, *outs):
    *blocks, sq_out, cols = outs
    params = (mult, offs, thr)
    n = len(SLOT_TILES[slot])
    for i in range(own.shape[0]):
        cols[i, 0:128, :] = own[i]
        for k, l in enumerate(SLOT_TILES[slot]):
            x = other[i, :, k * 128 : (k + 1) * 128]
            sq_out[i, k : k + 1, :] = sum_squares(x) + own_sq[i, l : l + 1, :]
            sample_into(cols, i, i, k, l, 1, x, salt, params)
        store_gram(slot, i, n, q, cols[i], blocks)


def gram_kernel0k(mine, other, q, salt, mult, offs, thr, keep, cols):
    for j in range(4):
        for k, l in enumerate(SLOT_TILES[0]):
            own = mine[4 + j, :, l * 128 : (l + 1) * 128].astype(jnp.float32)
            x = other[j, :, k * 128 : (k + 1) * 128]
            sample_into(cols, j, 4 + j, k, l, 0, own, salt, (mult, offs, thr))
            sample_into(cols, j, 4 + j, k, l, 1, x, salt, (mult, offs, thr))
        store_gram(0, 4 + j, 3, q, cols[j], (keep,))


def gram_kernel2(
    mine, other, q, salt, mult, offs, thr, sq_query, sq0s, other0k, sq1, send, keep, cols, extra
):
    for i in range(8):
        if i < 4:
            extra[i, 0:3, :] = sq0s[i, 0:3, :]
        else:
            for l in range(3):
                lanes = slice(l * 128, (l + 1) * 128)
                own = mine[i, :, lanes].astype(jnp.float32)
                extra[i, l : l + 1, :] = sum_squares(own) + sum_squares(other0k[i - 4, :, lanes])
        extra[i, 3:6, :] = sq1[i, 0:3, :]
        for k, l in enumerate(SLOT_TILES[2]):
            own = mine[i, :, l * 128 : (l + 1) * 128].astype(jnp.float32)
            x = other[i, :, k * 128 : (k + 1) * 128]
            extra[i, l : l + 1, :] = sum_squares(own) + sum_squares(x)
            sample_into(cols, i, i, k, l, 0, own, salt, (mult, offs, thr))
            sample_into(cols, i, i, k, l, 1, x, salt, (mult, offs, thr))
        store_gram(2, i, 2, q, cols[i], (send, keep), (extra[i], sq_query[...]))


def sample_into(cols, at, i, k, l, u, x, salt, params):
    core, _, tile = my_place()
    m, o, t = (ref[pl.ds(column_base(core, tile, i) + l, 1), :] for ref in params)
    users = slice(u * 128, (u + 1) * 128)
    value = sample(x, salt[users, :], m, o, t, weight_of(t))
    cols[at, users, k * 128 : (k + 1) * 128] = value


def store_gram(slot, i, n, q, cols, blocks, extra=None):
    xa, c, xb = ORDER[i]
    gram = jnp.dot(q[c], cols, preferred_element_type=jnp.float32)
    for group in range(8):
        ya, za, zb = group >> 2, group >> 1 & 1, group & 1
        near = (xa, ya, za)
        at = sum(near[(slot + k) % 3] << (5 - k) for k in range(1, 3))
        at += xb + (c ^ ya) * 2 + zb * 4
        ref = blocks[0] if near[slot] else blocks[-1]
        for k in range(n):
            ref[at, k * 32 : (k + 1) * 32, :] = gram[
                group * 32 : (group + 1) * 32, k * 128 : (k + 1) * 128
            ]
        if extra is not None:
            ref[at, 64:72, :] = extra[0]
            ref[at, 72:80, :] = extra[1]


def gram_call(slot, kernel, outs, operands):
    n = len(SLOT_TILES[slot])
    count = operands[1].shape[0]
    out_shape = [((32, SLOT_ROWS[slot], 128), jnp.float32)] * outs
    scratch = [pltpu.VMEM((count, 256, n * 128), jnp.bfloat16)]
    if slot == 2:
        scratch.append(pltpu.VMEM((8, 8, 128), jnp.float32))
    elif kernel is not gram_kernel0k:
        kernel = functools.partial(kernel, slot)
        out_shape.append(((count, 8, 128), jnp.float32))
    return call(
        kernel,
        out_shape,
        "v" * len(operands),
        scratch=scratch,
        flops=n * count * 16_000_000,
        nbytes=5 << 20,
    )(*operands)


def join_kernel(*refs):
    outs = refs[6:]
    for j in range(8):
        row = 0
        for slot in range(3):
            height = SLOT_ROWS[slot]
            outs[j][row : row + height, :] = refs[slot][j] + refs[3 + slot][j]
            row += height


def join_call(keeps, gots):
    return call(
        join_kernel, [((sum(SLOT_ROWS), 128), jnp.float32)] * 8, "v" * 6, limit=8, nbytes=4 << 20
    )(*keeps, *gots)


def last_sum_kernel(*refs):
    send, keep = refs[8:]
    core, _, _ = my_place()

    def total(start, height):
        parts = [ref[start : start + height, :] for ref in refs[:8]]
        return ((parts[0] + parts[1]) + (parts[2] + parts[3])) + (
            (parts[4] + parts[5]) + (parts[6] + parts[7])
        )

    for l in range(8):
        start = l * 32
        even, odd = total(start, 16), total(start + 16, 16)
        keep[l * 16 : (l + 1) * 16, :] = jnp.where(core == 0, even, odd)
        send[l * 16 : (l + 1) * 16, :] = jnp.where(core == 0, odd, even)
    squares = total(256, 8)
    send[128:136, :] = squares
    keep[128:136, :] = squares
    keep[136:144, :] = total(264, 8)


def last_sum_call(parts):
    return call(
        last_sum_kernel, [((136, 128), jnp.float32), ((144, 128), jnp.float32)], "v" * 8, limit=4
    )(*parts)


def finish_kernel(keep, other, out):
    core, pair, _ = my_place()
    row = pair * 2 + core
    line = jnp.broadcast_to(keep[pl.ds(136 + row // 8, 1), :], (16, 128))
    lane = lax.broadcasted_iota(jnp.int32, (16, 128), 1)
    spot = lax.broadcasted_iota(jnp.int32, (16, 128), 0) + (row % 8) * 16
    squares = jnp.sum(jnp.where(lane == spot, line, 0.0), axis=1, keepdims=True)
    query_norm = jnp.sqrt(squares + 1e-06)
    for source, half in ((keep, core), (other, 1 - core)):
        for l in range(8):
            norm = jnp.sqrt(source[128 + l : 129 + l, :] + 1e-06)
            at = pl.multiple_of(half * 1024 + l * 128, 128)
            out[:, pl.ds(at, 128)] = source[l * 16 : (l + 1) * 16, :] / (query_norm * norm)


def finish_call(keep, other):
    return call(finish_kernel, [((16, 2048), jnp.float32)], "vv", limit=4)(keep, other)[0]


def permute(x, pairs):
    return lax.ppermute(x, AXES, pairs)


def body(features, row_salt, column_multiplier, column_offset, thresholds):
    salt = row_salt.reshape(1, 128)
    params = [a.reshape(128, 128) for a in (column_multiplier, column_offset, thresholds)]
    partner = [(i, i ^ 8) for i in range(128)]
    other_salt = permute(salt, partner)
    xq, x0s, x1, x2, x0k, mine, queries = cast_call(features)
    yq = permute(xq, partner)
    y0s = permute(x0s, partner)
    y1 = permute(x1, partner)
    y2 = permute(x2, partner)
    y0k = permute(x0k, partner)
    own0s, own1, own_sq = own_call(mine, salt, *params)
    q, salts, sq_query = query_call(queries, yq, salt, other_salt, *params)
    common = (q, salts, *params)

    def gram(slot, kernel, outs, *operands):
        return gram_call(slot, kernel, outs, operands)

    send0, sq0s = gram(0, gram_kernel, 1, own0s, y0s, *common, own_sq)
    send1, keep1, sq1 = gram(1, gram_kernel, 2, own1, y1, *common, own_sq)
    send2, keep2 = gram(2, gram_kernel2, 2, mine, y2, *common, sq_query, sq0s, y0k, sq1)
    (keep0,) = gram(0, gram_kernel0k, 1, mine, y0k, *common)
    sends, keeps, gots = [send0, send1, send2], [keep0, keep1, keep2], [None] * 3
    none = [0, 0, 0]
    for step in range(3):
        half = 16 >> step
        for slot in range(3):
            got = permute(sends[slot], moves(axis_bits(slot + step), none))
            kept = keeps[slot]
            if step < 2:
                sends[slot] = kept[half:] + got[half:]
                keeps[slot] = kept[:half] + got[:half]
            else:
                gots[slot] = got
    chunks = join_call(keeps, gots)
    parts = [chunks[0]]
    for j in LAST:
        parts.append(permute(chunks[j], moves(none, [j & 1, j >> 1 & 1, j >> 2])))
    send, keep = last_sum_call(parts)
    return finish_call(keep, permute(send, partner))


LAST = (1, 2, 4, 3, 6, 5, 7)


def solution(mesh):
    placed = (P(AXES, None), P(AXES), P(), P(), P())
    return jax.shard_map(
        body, mesh=mesh, in_specs=placed, out_specs=P("rows", "tiles"), check_vma=False
    )
```

time: 98.5 us -> 79.6 us (0.81)
  waiting for transfers between devices: 47.5 us -> 35.8 us
  starting transfers between devices: 39.5 us -> 32.8 us
    ppermute x25 -> x23, waiting for transfers between devices: 47.5 us -> 35.8 us  [permute(): return lax.ppermute(x, AXES, pairs)]
    ppermute x25 -> x23, starting transfers between devices: 39.5 us -> 32.8 us  [permute(): return lax.ppermute(x, AXES, pairs)]
  transfers between devices with their start and end apart: 25 -> 23, of which waited for: 15 -> 12; matrix products, arithmetic and copies ran while one was open for 1% -> 1% of each run, Pallas kernels for 7% -> 8%
where the time goes in v3:
time: 79.6 us; the launch traced here: 79.5 us
  waiting for transfers between devices  35.8 us (45%)
  starting transfers between devices  32.8 us (41%)
  Pallas kernels  9.85 us (12%)
  other arithmetic  0.89 us (1%)
    ppermute x23, waiting for transfers between devices, permute(): return lax.ppermute(x, AXES, pairs)  35.8 us
    ppermute x23, starting transfers between devices, permute(): return lax.ppermute(x, AXES, pairs)  32.8 us
    pallas_call x4, Pallas kernels, gram_call(): call(kernel, out_shape, 'v' * len(operands), scratch=scratch, flops=n * c...  4.88 us
    pallas_call x1, Pallas kernels, cast_call(): call(cast_kernel, [((128, 256), f32), ((4, 128, 384), f32), ((8, 128, 384...  2.39 us
  transfers between devices with their start and end apart: 23, of which 12 were waited for; matrix products, arithmetic and copies ran while one was open for 1% of the time, Pallas kernels for 8%

profile of v3, /device:TPU:1, one launch (start us, length us, event | category | flops | bytes accessed | tf_op | source)
XLA Modules:
  0.0 79.5 jit_solution(1248293626706633895)
XLA Ops:
  0.0 2.4 %shard_map.55 = (f32[128,256]{1,0:T(8,128)S(1)}, f32[4,128,384]{2,1,0:T(8,128)S(1)}, f32[8,128,384]{2,1,0:T(8,128)S(1)}, f32[8,128,256]{2,1,0:T(8,128)S(1)}, f32...) custom-call(bf16[128,16384]{1,0:T(8,128)(2,1)} %feat.1), custom_call_target="tpu_custom_call" | custom-call | flops 1000000 | bytes 6291456 | tf_op jit(solution)/shard_map/pallas_call | solution.py:112
  2.4 1.4 %collective-permute-start.6 = (f32[8,128,384]{2,1,0:T(8,128)S(1)}, f32[8,128,384]{2,1,0:T(8,128)S(1)}, u32[]{:S(2)}, u32[]{:S(2)}) collective-permute-start(f32[8,128,384]{2,1,0:T(8,128)S(1)} %get-tuple-element.46), channel_id=1, source_target_pairs={{0,8},{1,9},{2,10},{3,11},{4,12},{5,13},{6,14},{7,15},{8,0},{9,1},... | collective-permute-start | bytes 4718600 | tf_op jit(solution)/shard_map/ppermute | solution.py:374
  3.9 0.1 collective-permute-start.3
  3.9 0.4 collective-permute-start.1
  4.4 0.1 collective-permute-start.9
  4.5 0.4 collective-permute-start.2
  4.9 1.3 %shard_map.58 = (bf16[4,128,384]{2,1,0:T(8,128)(2,1)S(1)}, bf16[8,128,384]{2,1,0:T(8,128)(2,1)S(1)}, f32[8,8,128]{2,1,0:T(8,128)S(1)}) custom-call(bf16[8,128,1024]{2,1,0:T(8,128)(2,1)S(1)} %get-tuple-element.35.mine, s32[1,128]{1,0:T(1,128)S(1)} %bitcast.23, s32[128,128]{1,0:T(8,128)S(1)} %bitcast.4, s32[128,128]{1,0:T(8,128)S(1)} %bitcast.10, ...), custom_call_target="tpu_custom_call" | custom-call | flops 12000000 | bytes 3145728 | tf_op jit(solution)/shard_map/pallas_call | solution.py:161
  6.2 3.5 %collective-permute-done.2.other_salt = s32[1,128]{1,0:T(1,128)S(1)} collective-permute-done((s32[1,128]{1,0:T(1,128)S(1)}, s32[1,128]{1,0:T(1,128)S(1)}, u32[]{:S(2)}, u32[]{:S(2)}) %collective-permute-start.2) | collective-permute-done | bytes 544 | tf_op jit(solution)/shard_map/ppermute | solution.py:374
  9.7 0.3 shard_map.56
  10.0 0.8 shard_map.59
  10.8 1.4 %collective-permute-start.4 = (f32[32,96,128]{2,1,0:T(8,128)S(1)}, f32[32,96,128]{2,1,0:T(8,128)S(1)}, u32[]{:S(2)}, u32[]{:S(2)}) collective-permute-start(f32[32,96,128]{2,1,0:T(8,128)S(1)} %get-tuple-element.44), channel_id=1, source_target_pairs={{0,3},{1,2},{2,1},{3,0},{4,7},{5,6},{6,5},{7,4},{8,9},{9,8},{10,11... | collective-permute-start | bytes 4718600 | tf_op jit(solution)/shard_map/ppermute | solution.py:374
  12.2 1.9 %collective-permute-start = (f32[4,128,384]{2,1,0:T(8,128)S(1)}, f32[4,128,384]{2,1,0:T(8,128)S(1)}, u32[]{:S(2)}, u32[]{:S(2)}) collective-permute-start(f32[4,128,384]{2,1,0:T(8,128)S(1)} %get-tuple-element.36), channel_id=1, source_target_pairs={{0,8},{1,9},{2,10},{3,11},{4,12},{5,13},{6,14},{7,15},{8,0},{9,1},... | collective-permute-start | bytes 2359304 | tf_op jit(solution)/shard_map/ppermute | solution.py:374
  14.1 1.3 %shard_map.60 = (f32[32,96,128]{2,1,0:T(8,128)S(1)}, f32[32,96,128]{2,1,0:T(8,128)S(1)}, f32[8,8,128]{2,1,0:T(8,128)S(1)}) custom-call(bf16[8,128,384]{2,1,0:T(8,128)(2,1)S(1)} %get-tuple-element.45.own, f32[8,128,384]{2,1,0:T(8,128)S(1)} %collective-permute-done.6.other, bf16[2,256,256]{2,1,0:T(8,128)(2,1)S(1)} %get-tuple-element.39.q, ...), custom_call_target="tpu_custom_call" | custom-call | flops 384000000 | bytes 5242880 | tf_op jit(solution)/shard_map/pallas_call | solution.py:301
  15.4 1.4 %collective-permute-start.7 = (f32[32,96,128]{2,1,0:T(8,128)S(1)}, f32[32,96,128]{2,1,0:T(8,128)S(1)}, u32[]{:S(2)}, u32[]{:S(2)}) collective-permute-start(f32[32,96,128]{2,1,0:T(8,128)S(1)} %get-tuple-element.48), channel_id=1, source_target_pairs={{0,68},{1,69},{2,70},{3,71},{4,64},{5,65},{6,66},{7,67},{8,12},{9,... | collective-permute-start | bytes 4718600 | tf_op jit(solution)/shard_map/ppermute | solution.py:374
  16.8 1.7 %shard_map.61 = (f32[32,80,128]{2,1,0:T(8,128)S(1)}, f32[32,80,128]{2,1,0:T(8,128)S(1)}) custom-call(bf16[8,128,1024]{2,1,0:T(8,128)(2,1)S(1)} %get-tuple-element.35.mine, f32[8,128,256]{2,1,0:T(8,128)S(1)} %collective-permute-done.9.other, bf16[2,256,256]{2,1,0:T(8,128)(2,1)S(1)} %get-tuple-element.39.q, s32[256,128]{1,0:T(8,128)S(1)} %get-tuple-element.40.salt, ...), custom_call_target="tpu_custom_call" | custom-call | flops 256000000 | bytes 5242880 | tf_op jit(solution)/shard_map/pallas_call | solution.py:301
  18.5 1.7 %collective-permute-start.10 = (f32[32,80,128]{2,1,0:T(8,128)S(1)}, f32[32,80,128]{2,1,0:T(8,128)S(1)}, u32[]{:S(2)}, u32[]{:S(2)}) collective-permute-start(f32[32,80,128]{2,1,0:T(8,128)S(1)} %get-tuple-element.54), channel_id=1, source_target_pairs={{0,48},{1,49},{2,50},{3,51},{4,52},{5,53},{6,54},{7,55},{8,24},{9,... | collective-permute-start | bytes 3932168 | tf_op jit(solution)/shard_map/ppermute | solution.py:374
  20.3 1.1 %shard_map.57 = f32[32,96,128]{2,1,0:T(8,128)S(1)} custom-call(bf16[8,128,1024]{2,1,0:T(8,128)(2,1)S(1)} %get-tuple-element.35.mine, f32[4,128,384]{2,1,0:T(8,128)S(1)} %collective-permute-done.other.other0k, bf16[2,256,256]{2,1,0:T(8,128)(2,1)S(1)} %get-tuple-element.39.q, s32[256,128]{1,0:T(8,128)S(1)} %get-tuple-element.40.salt, s32[128,128]{1,0:T(8,128)S(1)} %bitcast.9, ...), custom_call_target="tpu_custom_call" | custom-call | flops 192000000 | bytes 5242880 | tf_op jit(solution)/shard_map/pallas_call | solution.py:301
  21.4 9.0 %collective-permute-done.4 = f32[32,96,128]{2,1,0:T(8,128)S(1)} collective-permute-done((f32[32,96,128]{2,1,0:T(8,128)S(1)}, f32[32,96,128]{2,1,0:T(8,128)S(1)}, u32[]{:S(2)}, u32[]{:S(2)}) %collective-permute-start.4) | collective-permute-done | bytes 1572896 | tf_op jit(solution)/shard_map/ppermute | solution.py:374
  30.4 0.3 slice_add_fusion.3
  30.7 1.5 %collective-permute-start.5 = (f32[16,96,128]{2,1,0:T(8,128)S(1)}, f32[16,96,128]{2,1,0:T(8,128)S(1)}, u32[]{:S(2)}, u32[]{:S(2)}) collective-permute-start(f32[16,96,128]{2,1,0:T(8,128)S(1)} %get-tuple-element.68), channel_id=1, source_target_pairs={{0,68},{1,69},{2,70},{3,71},{4,64},{5,65},{6,66},{7,67},{8,12},{9,... | collective-permute-start | bytes 2359304 | tf_op jit(solution)/shard_map/ppermute | solution.py:374
  32.2 2.9 %collective-permute-done.7 = f32[32,96,128]{2,1,0:T(8,128)S(1)} collective-permute-done((f32[32,96,128]{2,1,0:T(8,128)S(1)}, f32[32,96,128]{2,1,0:T(8,128)S(1)}, u32[]{:S(2)}, u32[]{:S(2)}) %collective-permute-start.7) | collective-permute-done | bytes 1572896 | tf_op jit(solution)/shard_map/ppermute | solution.py:374
  35.1 0.2 slice_add_fusion.1
  35.3 1.7 %collective-permute-start.8 = (f32[16,96,128]{2,1,0:T(8,128)S(1)}, f32[16,96,128]{2,1,0:T(8,128)S(1)}, u32[]{:S(2)}, u32[]{:S(2)}) collective-permute-start(f32[16,96,128]{2,1,0:T(8,128)S(1)} %get-tuple-element.66), channel_id=1, source_target_pairs={{0,48},{1,49},{2,50},{3,51},{4,52},{5,53},{6,54},{7,55},{8,24},{9,... | collective-permute-start | bytes 2359304 | tf_op jit(solution)/shard_map/ppermute | solution.py:374
  37.0 0.1 slice_add_fusion.5
  37.1 0.1 collective-permute-start.11
  37.2 6.3 %collective-permute-done.5 = f32[16,96,128]{2,1,0:T(8,128)S(1)} collective-permute-done((f32[16,96,128]{2,1,0:T(8,128)S(1)}, f32[16,96,128]{2,1,0:T(8,128)S(1)}, u32[]{:S(2)}, u32[]{:S(2)}) %collective-permute-start.5) | collective-permute-done | bytes 786464 | tf_op jit(solution)/shard_map/ppermute | solution.py:374
  43.5 0.1 slice_add_fusion.7
  43.6 1.7 %collective-permute-start.12 = (f32[8,96,128]{2,1,0:T(8,128)S(1)}, f32[8,96,128]{2,1,0:T(8,128)S(1)}, u32[]{:S(2)}, u32[]{:S(2)}) collective-permute-start(f32[8,96,128]{2,1,0:T(8,128)S(1)} %get-tuple-element.73), channel_id=1, source_target_pairs={{0,48},{1,49},{2,50},{3,51},{4,52},{5,53},{6,54},{7,55},{8,24},{9,... | collective-permute-start | bytes 1179656 | tf_op jit(solution)/shard_map/ppermute | solution.py:374
  45.3 1.3 %collective-permute-done.8 = f32[16,96,128]{2,1,0:T(8,128)S(1)} collective-permute-done((f32[16,96,128]{2,1,0:T(8,128)S(1)}, f32[16,96,128]{2,1,0:T(8,128)S(1)}, u32[]{:S(2)}, u32[]{:S(2)}) %collective-permute-start.8) | collective-permute-done | bytes 786464 | tf_op jit(solution)/shard_map/ppermute | solution.py:374
  46.7 0.1 slice_add_fusion.6
  46.8 0.1 collective-permute-start.13
  47.0 1.4 %collective-permute-start.14 = (f32[8,80,128]{2,1,0:T(8,128)S(1)}, f32[8,80,128]{2,1,0:T(8,128)S(1)}, u32[]{:S(2)}, u32[]{:S(2)}) collective-permute-start(f32[8,80,128]{2,1,0:T(8,128)S(1)} %get-tuple-element.75), channel_id=1, source_target_pairs={{0,68},{1,69},{2,70},{3,71},{4,64},{5,65},{6,66},{7,67},{8,12},{9,... | collective-permute-start | bytes 983048 | tf_op jit(solution)/shard_map/ppermute | solution.py:374
  48.4 2.5 %collective-permute-done.12.refs_3_ = f32[8,96,128]{2,1,0:T(8,128)S(1)} collective-permute-done((f32[8,96,128]{2,1,0:T(8,128)S(1)}, f32[8,96,128]{2,1,0:T(8,128)S(1)}, u32[]{:S(2)}, u32[]{:S(2)}) %collective-permute-start.12) | collective-permute-done | bytes 393248 | tf_op jit(solution)/shard_map/ppermute | solution.py:374
  50.9 2.5 %collective-permute-done.14.refs_5_ = f32[8,80,128]{2,1,0:T(8,128)S(1)} collective-permute-done((f32[8,80,128]{2,1,0:T(8,128)S(1)}, f32[8,80,128]{2,1,0:T(8,128)S(1)}, u32[]{:S(2)}, u32[]{:S(2)}) %collective-permute-start.14) | collective-permute-done | bytes 327712 | tf_op jit(solution)/shard_map/ppermute | solution.py:374
  53.3 0.4 collective-permute-done.13.refs_4_
  53.8 0.1 shard_map.62
  53.9 0.4 collective-permute-start.15
  54.3 2.5 %collective-permute-start.16 = (f32[272,128]{1,0:T(8,128)S(1)}, f32[272,128]{1,0:T(8,128)S(1)}, u32[]{:S(2)}, u32[]{:S(2)}) collective-permute-start(f32[272,128]{1,0:T(8,128)S(1)} %get-tuple-element.57), channel_id=1, source_target_pairs={{0,4},{1,5},{2,6},{3,7},{4,0},{5,1},{6,2},{7,3},{8,76},{9,77},{10,... | collective-permute-start | bytes 417800 | tf_op jit(solution)/shard_map/ppermute | solution.py:374
  56.8 3.8 %collective-permute-start.17 = (f32[272,128]{1,0:T(8,128)S(1)}, f32[272,128]{1,0:T(8,128)S(1)}, u32[]{:S(2)}, u32[]{:S(2)}) collective-permute-start(f32[272,128]{1,0:T(8,128)S(1)} %get-tuple-element.58), channel_id=1, source_target_pairs={{0,16},{1,17},{2,18},{3,19},{4,20},{5,21},{6,22},{7,23},{8,56},{9,... | collective-permute-start | bytes 417800 | tf_op jit(solution)/shard_map/ppermute | solution.py:374
  60.6 2.1 %collective-permute-start.18 = (f32[272,128]{1,0:T(8,128)S(1)}, f32[272,128]{1,0:T(8,128)S(1)}, u32[]{:S(2)}, u32[]{:S(2)}) collective-permute-start(f32[272,128]{1,0:T(8,128)S(1)} %get-tuple-element.59), channel_id=1, source_target_pairs={{0,5},{1,4},{2,7},{3,6},{4,1},{5,0},{6,3},{7,2},{8,79},{9,78},{10,... | collective-permute-start | bytes 417800 | tf_op jit(solution)/shard_map/ppermute | solution.py:374
  62.7 2.4 %collective-permute-start.19 = (f32[272,128]{1,0:T(8,128)S(1)}, f32[272,128]{1,0:T(8,128)S(1)}, u32[]{:S(2)}, u32[]{:S(2)}) collective-permute-start(f32[272,128]{1,0:T(8,128)S(1)} %get-tuple-element.60), channel_id=1, source_target_pairs={{0,20},{1,21},{2,22},{3,23},{4,16},{5,17},{6,18},{7,19},{8,124},{9... | collective-permute-start | bytes 417800 | tf_op jit(solution)/shard_map/ppermute | solution.py:374
  65.1 2.7 %collective-permute-start.20 = (f32[272,128]{1,0:T(8,128)S(1)}, f32[272,128]{1,0:T(8,128)S(1)}, u32[]{:S(2)}, u32[]{:S(2)}) collective-permute-start(f32[272,128]{1,0:T(8,128)S(1)} %get-tuple-element.61), channel_id=1, source_target_pairs={{0,17},{1,16},{2,19},{3,18},{4,21},{5,20},{6,23},{7,22},{8,59},{9,... | collective-permute-start | bytes 417800 | tf_op jit(solution)/shard_map/ppermute | solution.py:374
  67.8 2.9 %collective-permute-start.21 = (f32[272,128]{1,0:T(8,128)S(1)}, f32[272,128]{1,0:T(8,128)S(1)}, u32[]{:S(2)}, u32[]{:S(2)}) collective-permute-start(f32[272,128]{1,0:T(8,128)S(1)} %get-tuple-element.62), channel_id=1, source_target_pairs={{0,21},{1,20},{2,23},{3,22},{4,17},{5,16},{6,19},{7,18},{8,127},{9... | collective-permute-start | bytes 417800 | tf_op jit(solution)/shard_map/ppermute | solution.py:374
  70.7 1.6 %collective-permute-done.20.refs_6_ = f32[272,128]{1,0:T(8,128)S(1)} collective-permute-done((f32[272,128]{1,0:T(8,128)S(1)}, f32[272,128]{1,0:T(8,128)S(1)}, u32[]{:S(2)}, u32[]{:S(2)}) %collective-permute-start.20) | collective-permute-done | bytes 139296 | tf_op jit(solution)/shard_map/ppermute | solution.py:374
  72.3 4.8 %collective-permute-done.21.refs_7_ = f32[272,128]{1,0:T(8,128)S(1)} collective-permute-done((f32[272,128]{1,0:T(8,128)S(1)}, f32[272,128]{1,0:T(8,128)S(1)}, u32[]{:S(2)}, u32[]{:S(2)}) %collective-permute-start.21) | collective-permute-done | bytes 139296 | tf_op jit(solution)/shard_map/ppermute | solution.py:374
  77.2 0.6 collective-permute-start.22
  77.8 0.9 %collective-permute-done.22.other = f32[136,128]{1,0:T(8,128)S(1)} collective-permute-done((f32[136,128]{1,0:T(8,128)S(1)}, f32[136,128]{1,0:T(8,128)S(1)}, u32[]{:S(2)}, u32[]{:S(2)}) %collective-permute-start.22) | collective-permute-done | bytes 69664 | tf_op jit(solution)/shard_map/ppermute | solution.py:374
  78.7 0.8 shard_map.64
  (22 shorter events, 0.3 us)
Async XLA Ops:
  0.0 4.5 %copy-start.3 = (s32[128]{0:T(128)S(1)}, s32[128]{0:T(128)}, u32[]{:S(2)}) copy-start(s32[128]{0:T(128)} %param.6) | copy-start | bytes 1540
  0.0 4.9 %copy-start = (s32[16384]{0:T(1024)S(1)}, s32[16384]{0:T(1024)}, u32[]{:S(2)}) copy-start(s32[16384]{0:T(1024)} %param.7) | copy-start | bytes 196612
  0.0 4.9 %copy-start.1 = (s32[16384]{0:T(1024)S(1)}, s32[16384]{0:T(1024)}, u32[]{:S(2)}) copy-start(s32[16384]{0:T(1024)} %param.8) | copy-start | bytes 196612
  0.0 4.9 %copy-start.2 = (s32[16384]{0:T(1024)S(1)}, s32[16384]{0:T(1024)}, u32[]{:S(2)}) copy-start(s32[16384]{0:T(1024)} %param.9) | copy-start | bytes 196612
  2.4 11.7 %collective-permute-start.6 = (f32[8,128,384]{2,1,0:T(8,128)S(1)}, f32[8,128,384]{2,1,0:T(8,128)S(1)}, u32[]{:S(2)}, u32[]{:S(2)}) collective-permute-start(f32[8,128,384]{2,1,0:T(8,128)S(1)} %get-tuple-element.46), channel_id=1, source_target_pairs={{0,8},{1,9},{2,10},{3,11},{4,12},{5,13},{6,14},{7,15},{8,0},{9,1},... | collective-permute-start | bytes 4718600 | tf_op jit(solution)/shard_map/ppermute | solution.py:374
  3.9 6.1 %collective-permute-start.3 = (f32[4,128,384]{2,1,0:T(8,128)S(1)}, f32[4,128,384]{2,1,0:T(8,128)S(1)}, u32[]{:S(2)}, u32[]{:S(2)}) collective-permute-start(f32[4,128,384]{2,1,0:T(8,128)S(1)} %get-tuple-element.42), channel_id=1, source_target_pairs={{0,8},{1,9},{2,10},{3,11},{4,12},{5,13},{6,14},{7,15},{8,0},{9,1},... | collective-permute-start | bytes 2359304 | tf_op jit(solution)/shard_map/ppermute | solution.py:374
  3.9 5.8 %collective-permute-start.1 = (f32[128,256]{1,0:T(8,128)S(1)}, f32[128,256]{1,0:T(8,128)S(1)}, u32[]{:S(2)}, u32[]{:S(2)}) collective-permute-start(f32[128,256]{1,0:T(8,128)S(1)} %get-tuple-element.38), channel_id=1, source_target_pairs={{0,8},{1,9},{2,10},{3,11},{4,12},{5,13},{6,14},{7,15},{8,0},{9,1},... | collective-permute-start | bytes 393224 | tf_op jit(solution)/shard_map/ppermute | solution.py:374
  4.4 12.5 %collective-permute-start.9 = (f32[8,128,256]{2,1,0:T(8,128)S(1)}, f32[8,128,256]{2,1,0:T(8,128)S(1)}, u32[]{:S(2)}, u32[]{:S(2)}) collective-permute-start(f32[8,128,256]{2,1,0:T(8,128)S(1)} %get-tuple-element.49), channel_id=1, source_target_pairs={{0,8},{1,9},{2,10},{3,11},{4,12},{5,13},{6,14},{7,15},{8,0},{9,1},... | collective-permute-start | bytes 3145736 | tf_op jit(solution)/shard_map/ppermute | solution.py:374
  4.5 5.2 %collective-permute-start.2 = (s32[1,128]{1,0:T(1,128)S(1)}, s32[1,128]{1,0:T(1,128)S(1)}, u32[]{:S(2)}, u32[]{:S(2)}) collective-permute-start(s32[1,128]{1,0:T(1,128)S(1)} %bitcast.22), channel_id=1, source_target_pairs={{0,8},{1,9},{2,10},{3,11},{4,12},{5,13},{6,14},{7,15},{8,0},{9,1},... | collective-permute-start | bytes 1544 | tf_op jit(solution)/shard_map/ppermute | solution.py:374
  10.8 19.6 %collective-permute-start.4 = (f32[32,96,128]{2,1,0:T(8,128)S(1)}, f32[32,96,128]{2,1,0:T(8,128)S(1)}, u32[]{:S(2)}, u32[]{:S(2)}) collective-permute-start(f32[32,96,128]{2,1,0:T(8,128)S(1)} %get-tuple-element.44), channel_id=1, source_target_pairs={{0,3},{1,2},{2,1},{3,0},{4,7},{5,6},{6,5},{7,4},{8,9},{9,8},{10,11... | collective-permute-start | bytes 4718600 | tf_op jit(solution)/shard_map/ppermute | solution.py:374
  12.2 4.6 %collective-permute-start = (f32[4,128,384]{2,1,0:T(8,128)S(1)}, f32[4,128,384]{2,1,0:T(8,128)S(1)}, u32[]{:S(2)}, u32[]{:S(2)}) collective-permute-start(f32[4,128,384]{2,1,0:T(8,128)S(1)} %get-tuple-element.36), channel_id=1, source_target_pairs={{0,8},{1,9},{2,10},{3,11},{4,12},{5,13},{6,14},{7,15},{8,0},{9,1},... | collective-permute-start | bytes 2359304 | tf_op jit(solution)/shard_map/ppermute | solution.py:374
  15.4 19.6 %collective-permute-start.7 = (f32[32,96,128]{2,1,0:T(8,128)S(1)}, f32[32,96,128]{2,1,0:T(8,128)S(1)}, u32[]{:S(2)}, u32[]{:S(2)}) collective-permute-start(f32[32,96,128]{2,1,0:T(8,128)S(1)} %get-tuple-element.48), channel_id=1, source_target_pairs={{0,68},{1,69},{2,70},{3,71},{4,64},{5,65},{6,66},{7,67},{8,12},{9,... | collective-permute-start | bytes 4718600 | tf_op jit(solution)/shard_map/ppermute | solution.py:374
  18.5 18.4 %collective-permute-start.10 = (f32[32,80,128]{2,1,0:T(8,128)S(1)}, f32[32,80,128]{2,1,0:T(8,128)S(1)}, u32[]{:S(2)}, u32[]{:S(2)}) collective-permute-start(f32[32,80,128]{2,1,0:T(8,128)S(1)} %get-tuple-element.54), channel_id=1, source_target_pairs={{0,48},{1,49},{2,50},{3,51},{4,52},{5,53},{6,54},{7,55},{8,24},{9,... | collective-permute-start | bytes 3932168 | tf_op jit(solution)/shard_map/ppermute | solution.py:374
  30.7 12.9 %collective-permute-start.5 = (f32[16,96,128]{2,1,0:T(8,128)S(1)}, f32[16,96,128]{2,1,0:T(8,128)S(1)}, u32[]{:S(2)}, u32[]{:S(2)}) collective-permute-start(f32[16,96,128]{2,1,0:T(8,128)S(1)} %get-tuple-element.68), channel_id=1, source_target_pairs={{0,68},{1,69},{2,70},{3,71},{4,64},{5,65},{6,66},{7,67},{8,12},{9,... | collective-permute-start | bytes 2359304 | tf_op jit(solution)/shard_map/ppermute | solution.py:374
  35.3 11.4 %collective-permute-start.8 = (f32[16,96,128]{2,1,0:T(8,128)S(1)}, f32[16,96,128]{2,1,0:T(8,128)S(1)}, u32[]{:S(2)}, u32[]{:S(2)}) collective-permute-start(f32[16,96,128]{2,1,0:T(8,128)S(1)} %get-tuple-element.66), channel_id=1, source_target_pairs={{0,48},{1,49},{2,50},{3,51},{4,52},{5,53},{6,54},{7,55},{8,24},{9,... | collective-permute-start | bytes 2359304 | tf_op jit(solution)/shard_map/ppermute | solution.py:374
  37.1 9.8 %collective-permute-start.11 = (f32[16,80,128]{2,1,0:T(8,128)S(1)}, f32[16,80,128]{2,1,0:T(8,128)S(1)}, u32[]{:S(2)}, u32[]{:S(2)}) collective-permute-start(f32[16,80,128]{2,1,0:T(8,128)S(1)} %get-tuple-element.70), channel_id=1, source_target_pairs={{0,3},{1,2},{2,1},{3,0},{4,7},{5,6},{6,5},{7,4},{8,9},{9,8},{10,11... | collective-permute-start | bytes 1966088 | tf_op jit(solution)/shard_map/ppermute | solution.py:374
  43.6 7.3 %collective-permute-start.12 = (f32[8,96,128]{2,1,0:T(8,128)S(1)}, f32[8,96,128]{2,1,0:T(8,128)S(1)}, u32[]{:S(2)}, u32[]{:S(2)}) collective-permute-start(f32[8,96,128]{2,1,0:T(8,128)S(1)} %get-tuple-element.73), channel_id=1, source_target_pairs={{0,48},{1,49},{2,50},{3,51},{4,52},{5,53},{6,54},{7,55},{8,24},{9,... | collective-permute-start | bytes 1179656 | tf_op jit(solution)/shard_map/ppermute | solution.py:374
  46.8 7.0 %collective-permute-start.13 = (f32[8,96,128]{2,1,0:T(8,128)S(1)}, f32[8,96,128]{2,1,0:T(8,128)S(1)}, u32[]{:S(2)}, u32[]{:S(2)}) collective-permute-start(f32[8,96,128]{2,1,0:T(8,128)S(1)} %get-tuple-element.71), channel_id=1, source_target_pairs={{0,3},{1,2},{2,1},{3,0},{4,7},{5,6},{6,5},{7,4},{8,9},{9,8},{10,11... | collective-permute-start | bytes 1179656 | tf_op jit(solution)/shard_map/ppermute | solution.py:374
  47.0 6.3 %collective-permute-start.14 = (f32[8,80,128]{2,1,0:T(8,128)S(1)}, f32[8,80,128]{2,1,0:T(8,128)S(1)}, u32[]{:S(2)}, u32[]{:S(2)}) collective-permute-start(f32[8,80,128]{2,1,0:T(8,128)S(1)} %get-tuple-element.75), channel_id=1, source_target_pairs={{0,68},{1,69},{2,70},{3,71},{4,64},{5,65},{6,66},{7,67},{8,12},{9,... | collective-permute-start | bytes 983048 | tf_op jit(solution)/shard_map/ppermute | solution.py:374
  53.9 11.2 %collective-permute-start.15 = (f32[272,128]{1,0:T(8,128)S(1)}, f32[272,128]{1,0:T(8,128)S(1)}, u32[]{:S(2)}, u32[]{:S(2)}) collective-permute-start(f32[272,128]{1,0:T(8,128)S(1)} %get-tuple-element.56), channel_id=1, source_target_pairs={{0,1},{1,0},{2,3},{3,2},{4,5},{5,4},{6,7},{7,6},{8,11},{9,10},{10,... | collective-permute-start | bytes 417800 | tf_op jit(solution)/shard_map/ppermute | solution.py:374
  54.3 13.5 %collective-permute-start.16 = (f32[272,128]{1,0:T(8,128)S(1)}, f32[272,128]{1,0:T(8,128)S(1)}, u32[]{:S(2)}, u32[]{:S(2)}) collective-permute-start(f32[272,128]{1,0:T(8,128)S(1)} %get-tuple-element.57), channel_id=1, source_target_pairs={{0,4},{1,5},{2,6},{3,7},{4,0},{5,1},{6,2},{7,3},{8,76},{9,77},{10,... | collective-permute-start | bytes 417800 | tf_op jit(solution)/shard_map/ppermute | solution.py:374
  56.8 13.9 %collective-permute-start.17 = (f32[272,128]{1,0:T(8,128)S(1)}, f32[272,128]{1,0:T(8,128)S(1)}, u32[]{:S(2)}, u32[]{:S(2)}) collective-permute-start(f32[272,128]{1,0:T(8,128)S(1)} %get-tuple-element.58), channel_id=1, source_target_pairs={{0,16},{1,17},{2,18},{3,19},{4,20},{5,21},{6,22},{7,23},{8,56},{9,... | collective-permute-start | bytes 417800 | tf_op jit(solution)/shard_map/ppermute | solution.py:374
  60.6 10.1 %collective-permute-start.18 = (f32[272,128]{1,0:T(8,128)S(1)}, f32[272,128]{1,0:T(8,128)S(1)}, u32[]{:S(2)}, u32[]{:S(2)}) collective-permute-start(f32[272,128]{1,0:T(8,128)S(1)} %get-tuple-element.59), channel_id=1, source_target_pairs={{0,5},{1,4},{2,7},{3,6},{4,1},{5,0},{6,3},{7,2},{8,79},{9,78},{10,... | collective-permute-start | bytes 417800 | tf_op jit(solution)/shard_map/ppermute | solution.py:374
  62.7 8.0 %collective-permute-start.19 = (f32[272,128]{1,0:T(8,128)S(1)}, f32[272,128]{1,0:T(8,128)S(1)}, u32[]{:S(2)}, u32[]{:S(2)}) collective-permute-start(f32[272,128]{1,0:T(8,128)S(1)} %get-tuple-element.60), channel_id=1, source_target_pairs={{0,20},{1,21},{2,22},{3,23},{4,16},{5,17},{6,18},{7,19},{8,124},{9... | collective-permute-start | bytes 417800 | tf_op jit(solution)/shard_map/ppermute | solution.py:374
  65.1 7.2 %collective-permute-start.20 = (f32[272,128]{1,0:T(8,128)S(1)}, f32[272,128]{1,0:T(8,128)S(1)}, u32[]{:S(2)}, u32[]{:S(2)}) collective-permute-start(f32[272,128]{1,0:T(8,128)S(1)} %get-tuple-element.61), channel_id=1, source_target_pairs={{0,17},{1,16},{2,19},{3,18},{4,21},{5,20},{6,23},{7,22},{8,59},{9,... | collective-permute-start | bytes 417800 | tf_op jit(solution)/shard_map/ppermute | solution.py:374
  67.8 9.3 %collective-permute-start.21 = (f32[272,128]{1,0:T(8,128)S(1)}, f32[272,128]{1,0:T(8,128)S(1)}, u32[]{:S(2)}, u32[]{:S(2)}) collective-permute-start(f32[272,128]{1,0:T(8,128)S(1)} %get-tuple-element.62), channel_id=1, source_target_pairs={{0,21},{1,20},{2,23},{3,22},{4,17},{5,16},{6,19},{7,18},{8,127},{9... | collective-permute-start | bytes 417800 | tf_op jit(solution)/shard_map/ppermute | solution.py:374
  77.2 1.5 %collective-permute-start.22 = (f32[136,128]{1,0:T(8,128)S(1)}, f32[136,128]{1,0:T(8,128)S(1)}, u32[]{:S(2)}, u32[]{:S(2)}) collective-permute-start(f32[136,128]{1,0:T(8,128)S(1)} %get-tuple-element.64), channel_id=1, source_target_pairs={{0,8},{1,9},{2,10},{3,11},{4,12},{5,13},{6,14},{7,15},{8,0},{9,1},... | collective-permute-start | bytes 208904 | tf_op jit(solution)/shard_map/ppermute | solution.py:374
